TPU v7x, 1024 devices: a whole 4x4x32 slice. The times are simulated.
1024 devices in a mesh: lat: 16 (over x, y), lon: 64 (over z, core).
Axes of the slice: x: 4, y: 4, z: 32, core: 2. Of those that a mesh axis runs over, the one named last changes fastest.
Arguments:
- pressure: float32 [16, 30, 40960], P('lat', None, 'lon'), may hold values from -6 to 6
- velocity: float32 [16, 30, 61440], P('lat', None, 'lon'), may hold values from -6 to 6
- edge_cells: int32 [16, 2, 61440], P('lat', None, 'lon'), may hold values from 0 to 1663
- cell_edges: int32 [16, 3, 40960], P('lat', None, 'lon'), may hold values from 0 to 1983
- send_cells: int32 [16, 8, 8192], P('lat', None, 'lon'), may hold values from 0 to 639
- send_edges: int32 [16, 8, 8192], P('lat', None, 'lon'), may hold values from 0 to 959
- inv_dual: float32 [16, 61440], P('lat', 'lon'), may hold values from 0.5 to 2
- edge_weight: float32 [16, 3, 40960], P('lat', None, 'lon'), may hold values from -3 to 3
- sound_speed: float32 [16, 40960], P('lat', 'lon'), may hold values from 0.1 to 0.6
- coupling: float32 [16, 30, 40960], P('lat', None, 'lon'), may hold values from 0.1 to 2
Outputs:
- pressure_out: float32 [16, 30, 40960], P('lat', None, 'lon')
- velocity_out: float32 [16, 30, 61440], P('lat', None, 'lon')
Inputs may be any that keep to these rules, and one draw needn't show every extreme that they name: `edge_cells`: positions below 640 are own cells; position 640 + r * 128 + j is slot j of the halo piece from the neighbour at offset number r. `cell_edges`: positions below 960 are own edges; position 960 + r * 128 + j is slot j of the edge halo piece from the neighbour at offset number r. `send_cells`: indices of own cells. `send_edges`: indices of own edges.
All inputs are finite; a program needn't handle non-finite values.
Results may differ from a plain program's by a relative error of at most 0.0001.
Values sent between devices are 32-bit elements; how exact they have to be, the bound alone decides.
A program may use at most 64 MiB of HBM per device.

v0:
```python
import jax
import jax.numpy as jnp
from jax import lax
from jax.sharding import PartitionSpec as P

NSUB = 3


DIRECTIONS = ((-1, -1), (-1, 0), (-1, 1), (0, -1), (0, 1), (1, -1), (1, 0), (1, 1))
step_scale = 0.5


def from_behind(block, axis, distance):
    devices = range(lax.axis_size(axis))
    route = [((i - distance) % len(devices), i) for i in devices]
    return lax.ppermute(block, axis, route)


def passed_along(value, axis, steps):
    count = lax.axis_size(axis)
    first, last = (max(0, -steps), min(count, count - steps))
    return lax.ppermute(value, axis, [(source, source + steps) for source in range(first, last)])


def position(offset):
    return DIRECTIONS.index(offset)


def edge_update(normal, extended, edge_cells, inv_dual):
    gradient = (
        jnp.take(extended, edge_cells[1], axis=1) - jnp.take(extended, edge_cells[0], axis=1)
    ) * inv_dual[None, :]
    return normal - step_scale * gradient


def column_solve(right_side, coupling):
    levels = right_side.shape[0]
    ratios = []
    scaled = []
    for level_index in range(levels):
        if level_index < levels - 1:
            upper_term = -coupling[level_index]
        else:
            upper_term = 0.0 * coupling[0]
        if level_index == 0:
            divisor = 1.0 + coupling[0]
            current = right_side[0] / divisor
        else:
            lower_term = -coupling[level_index - 1]
            diagonal = 1.0 + coupling[level_index - 1] + coupling[level_index]
            divisor = diagonal - lower_term * ratios[-1]
            current = (right_side[level_index] - lower_term * scaled[-1]) / divisor
        ratios.append(upper_term / divisor)
        scaled.append(current)
    result = [scaled[-1]]
    for level_index in range(levels - 2, -1, -1):
        result.insert(0, scaled[level_index] - ratios[level_index] * result[0])
    return jnp.stack(result)


def cell_update(values, edges_ext, cell_edges, edge_weight, sound_speed, coupling):
    divergence = jnp.take(edges_ext, cell_edges[0], axis=1) * edge_weight[0][None, :]
    divergence = divergence + jnp.take(edges_ext, cell_edges[1], axis=1) * edge_weight[1][None, :]
    divergence = divergence + jnp.take(edges_ext, cell_edges[2], axis=1) * edge_weight[2][None, :]
    right_side = values - sound_speed[None, :] * divergence
    return column_solve(right_side, coupling)


def extend(source, send_list):
    buffers = [jnp.take(source, send_list[member], axis=1) for member in range(8)]
    received = {}
    passing = {}
    for lon_step in (1, -1):
        bundle = jnp.stack([buffers[position((lat_step, lon_step))] for lat_step in (-1, 0, 1)])
        arrived = from_behind(bundle, "lon", lon_step)
        received[0, -lon_step] = arrived[1]
        passing[-1, lon_step] = arrived[0]
        passing[1, lon_step] = arrived[2]
    for lat_step in (1, -1):
        bundle = jnp.stack(
            [passing[lat_step, -1], buffers[position((lat_step, 0))], passing[lat_step, 1]]
        )
        arrived = passed_along(bundle, "lat", lat_step)
        for member, lon_step in enumerate((-1, 0, 1)):
            received[-lat_step, -lon_step] = arrived[member]
    return jnp.concatenate([source] + [received[offset] for offset in DIRECTIONS], axis=1)


def on_device(
    pressure,
    velocity,
    edge_cells,
    cell_edges,
    send_cells,
    send_edges,
    inv_dual,
    edge_weight,
    sound_speed,
    coupling,
):
    values = pressure[0]
    normal = velocity[0]
    for substep in range(NSUB):
        extended = extend(values, send_cells[0])
        normal = edge_update(normal, extended, edge_cells[0], inv_dual[0])
        edges_ext = extend(normal, send_edges[0])
        values = cell_update(
            values, edges_ext, cell_edges[0], edge_weight[0], sound_speed[0], coupling[0]
        )
    return (values[None], normal[None])


def solution(mesh):
    return jax.shard_map(
        on_device,
        mesh=mesh,
        in_specs=(
            P("lat", None, "lon"),
            P("lat", None, "lon"),
            P("lat", None, "lon"),
            P("lat", None, "lon"),
            P("lat", None, "lon"),
            P("lat", None, "lon"),
            P("lat", "lon"),
            P("lat", None, "lon"),
            P("lat", "lon"),
            P("lat", None, "lon"),
        ),
        out_specs=(P("lat", None, "lon"), P("lat", None, "lon")),
        check_vma=False,
    )
```

profile of v0, /device:TPU:6, one launch (start us, length us, event | category | flops | bytes accessed | tf_op | source)
XLA Modules:
  0.0 215.5 jit_solution(7298309071377822468)
XLA Ops:
  6.5 16.2 %collective-permute-start = (f32[3,30,128]{2,1,0:T(8,128)S(1)}, f32[3,30,128]{2,1,0:T(8,128)S(1)}, u32[]{:S(2)}, u32[]{:S(2)}) collective-permute-start(f32[3,30,128]{2,1,0:T(8,128)S(1)} %pad_maximum_fusion.12), channel_id=1, source_target_pairs={{1,0},{2,1},{3,2},{4,3},{5,4},{6,5},{7,6},{8,7},{9,8},{10,9},{11,1... | collective-permute-start | bytes 138248 | tf_op jit(solution)/shard_map/ppermute | solution.py:16
  29.8 3.5 %collective-permute-start.2 = (f32[3,30,128]{2,1,0:T(8,128)S(1)}, f32[3,30,128]{2,1,0:T(8,128)S(1)}, u32[]{:S(2)}, u32[]{:S(2)}) collective-permute-start(f32[3,30,128]{2,1,0:T(8,128)S(1)} %pad_maximum_fusion.14), channel_id=1, source_target_pairs={{0,64},{64,128},{128,192},{192,256},{256,320},{320,384},{384,448},... | collective-permute-start | bytes 138248 | tf_op jit(solution)/shard_map/ppermute | solution.py:22
  33.3 4.5 %collective-permute-start.3 = (f32[3,30,128]{2,1,0:T(8,128)S(1)}, f32[3,30,128]{2,1,0:T(8,128)S(1)}, u32[]{:S(2)}, u32[]{:S(2)}) collective-permute-start(f32[3,30,128]{2,1,0:T(8,128)S(1)} %pad_maximum_fusion.15), channel_id=1, source_target_pairs={{64,0},{128,64},{192,128},{256,192},{320,256},{384,320},{448,384},... | collective-permute-start | bytes 138248 | tf_op jit(solution)/shard_map/ppermute | solution.py:22
  37.9 1.6 collective-permute-done.3
  39.8 2.9 %gather_fusion.9 = f32[960,30]{1,0:T(8,128)S(1)} fusion(f32[30,1664]{0,1:T(8,128)S(1)} %copy.911, s32[1024]{0:T(1024)S(1)} %pad_clamp_fusion.11), kind=kCustom, calls=%fused_computation.27.clone | custom fusion | bytes 234240 | tf_op jit(solution)/shard_map/jit(_take)/gather | solution.py:31
  42.7 2.9 %gather_fusion.8 = f32[960,30]{1,0:T(8,128)S(1)} fusion(f32[30,1664]{0,1:T(8,128)S(1)} %copy.911, s32[1024]{0:T(1024)S(1)} %pad_clamp_fusion.12), kind=kCustom, calls=%fused_computation.1.clone | custom fusion | bytes 234240 | tf_op jit(solution)/shard_map/jit(_take)/gather | solution.py:31
  51.8 2.9 %collective-permute-start.4 = (f32[3,30,128]{1,2,0:T(8,128)S(1)}, f32[3,30,128]{1,2,0:T(8,128)S(1)}, u32[]{:S(2)}, u32[]{:S(2)}) collective-permute-start(f32[3,30,128]{1,2,0:T(8,128)S(1)} %pad_maximum_fusion), channel_id=1, source_target_pairs={{1,0},{2,1},{3,2},{4,3},{5,4},{6,5},{7,6},{8,7},{9,8},{10,9},{11,1... | collective-permute-start | bytes 138248 | tf_op jit(solution)/shard_map/ppermute | solution.py:16
  55.6 2.3 %collective-permute-done.4 = f32[3,30,128]{1,2,0:T(8,128)S(1)} collective-permute-done((f32[3,30,128]{1,2,0:T(8,128)S(1)}, f32[3,30,128]{1,2,0:T(8,128)S(1)}, u32[]{:S(2)}, u32[]{:S(2)}) %collective-permute-start.4) | collective-permute-done | bytes 46112 | tf_op jit(solution)/shard_map/ppermute | solution.py:16
  58.0 3.3 %collective-permute-start.6 = (f32[3,30,128]{1,2,0:T(8,128)S(1)}, f32[3,30,128]{1,2,0:T(8,128)S(1)}, u32[]{:S(2)}, u32[]{:S(2)}) collective-permute-start(f32[3,30,128]{1,2,0:T(8,128)S(1)} %pad_maximum_fusion.2), channel_id=1, source_target_pairs={{0,64},{64,128},{128,192},{192,256},{256,320},{320,384},{384,448},... | collective-permute-start | bytes 138248 | tf_op jit(solution)/shard_map/ppermute | solution.py:22
  61.3 5.0 %collective-permute-start.7 = (f32[3,30,128]{1,2,0:T(8,128)S(1)}, f32[3,30,128]{1,2,0:T(8,128)S(1)}, u32[]{:S(2)}, u32[]{:S(2)}) collective-permute-start(f32[3,30,128]{1,2,0:T(8,128)S(1)} %pad_maximum_fusion.3), channel_id=1, source_target_pairs={{64,0},{128,64},{192,128},{256,192},{320,256},{384,320},{448,384},... | collective-permute-start | bytes 138248 | tf_op jit(solution)/shard_map/ppermute | solution.py:22
  66.3 1.7 collective-permute-done.6
  68.0 1.4 collective-permute-done.7
  69.5 1.7 gather_fusion.20
  71.3 1.7 gather_fusion.19
  73.1 1.7 gather_fusion.18
  90.8 2.9 %collective-permute-start.8 = (f32[3,30,128]{2,1,0:T(8,128)S(1)}, f32[3,30,128]{2,1,0:T(8,128)S(1)}, u32[]{:S(2)}, u32[]{:S(2)}) collective-permute-start(f32[3,30,128]{2,1,0:T(8,128)S(1)} %pad_maximum_fusion.16), channel_id=1, source_target_pairs={{1,0},{2,1},{3,2},{4,3},{5,4},{6,5},{7,6},{8,7},{9,8},{10,9},{11,1... | collective-permute-start | bytes 138248 | tf_op jit(solution)/shard_map/ppermute | solution.py:16
  93.7 1.7 collective-permute-done.8
  95.4 2.3 %collective-permute-start.10 = (f32[3,30,128]{2,1,0:T(8,128)S(1)}, f32[3,30,128]{2,1,0:T(8,128)S(1)}, u32[]{:S(2)}, u32[]{:S(2)}) collective-permute-start(f32[3,30,128]{2,1,0:T(8,128)S(1)} %pad_maximum_fusion.18), channel_id=1, source_target_pairs={{0,64},{64,128},{128,192},{192,256},{256,320},{320,384},{384,448},... | collective-permute-start | bytes 138248 | tf_op jit(solution)/shard_map/ppermute | solution.py:22
  97.7 5.8 %collective-permute-start.11 = (f32[3,30,128]{2,1,0:T(8,128)S(1)}, f32[3,30,128]{2,1,0:T(8,128)S(1)}, u32[]{:S(2)}, u32[]{:S(2)}) collective-permute-start(f32[3,30,128]{2,1,0:T(8,128)S(1)} %pad_maximum_fusion.19), channel_id=1, source_target_pairs={{64,0},{128,64},{192,128},{256,192},{320,256},{384,320},{448,384},... | collective-permute-start | bytes 138248 | tf_op jit(solution)/shard_map/ppermute | solution.py:22
  103.7 1.6 collective-permute-done.11
  105.7 2.9 %gather_fusion.30 = f32[960,30]{1,0:T(8,128)S(1)} fusion(f32[30,1664]{0,1:T(8,128)S(1)} %copy.932, s32[1024]{0:T(1024)S(1)} %pad_clamp_fusion.11), kind=kCustom, calls=%fused_computation.29.clone | custom fusion | bytes 234240 | tf_op jit(solution)/shard_map/jit(_take)/gather | solution.py:31
  108.6 2.9 %gather_fusion.29 = f32[960,30]{1,0:T(8,128)S(1)} fusion(f32[30,1664]{0,1:T(8,128)S(1)} %copy.932, s32[1024]{0:T(1024)S(1)} %pad_clamp_fusion.12), kind=kCustom, calls=%fused_computation.28.clone | custom fusion | bytes 234240 | tf_op jit(solution)/shard_map/jit(_take)/gather | solution.py:31
  121.9 2.4 %collective-permute-start.12 = (f32[3,30,128]{1,2,0:T(8,128)S(1)}, f32[3,30,128]{1,2,0:T(8,128)S(1)}, u32[]{:S(2)}, u32[]{:S(2)}) collective-permute-start(f32[3,30,128]{1,2,0:T(8,128)S(1)} %pad_maximum_fusion.4), channel_id=1, source_target_pairs={{1,0},{2,1},{3,2},{4,3},{5,4},{6,5},{7,6},{8,7},{9,8},{10,9},{11,1... | collective-permute-start | bytes 138248 | tf_op jit(solution)/shard_map/ppermute | solution.py:16
  124.5 1.7 collective-permute-done.13
  126.2 1.3 collective-permute-done.12
  127.6 1.9 collective-permute-start.14
  129.5 6.5 %collective-permute-start.15 = (f32[3,30,128]{1,2,0:T(8,128)S(1)}, f32[3,30,128]{1,2,0:T(8,128)S(1)}, u32[]{:S(2)}, u32[]{:S(2)}) collective-permute-start(f32[3,30,128]{1,2,0:T(8,128)S(1)} %pad_maximum_fusion.7), channel_id=1, source_target_pairs={{64,0},{128,64},{192,128},{256,192},{320,256},{384,320},{448,384},... | collective-permute-start | bytes 138248 | tf_op jit(solution)/shard_map/ppermute | solution.py:22
  136.1 1.5 collective-permute-done.14
  137.7 1.4 collective-permute-done.15
  139.1 1.7 gather_fusion.41
  140.8 1.7 gather_fusion.40
  142.5 1.7 gather_fusion.39
  156.1 3.0 %collective-permute-start.16 = (f32[3,30,128]{2,1,0:T(8,128)S(1)}, f32[3,30,128]{2,1,0:T(8,128)S(1)}, u32[]{:S(2)}, u32[]{:S(2)}) collective-permute-start(f32[3,30,128]{2,1,0:T(8,128)S(1)} %pad_maximum_fusion.20), channel_id=1, source_target_pairs={{1,0},{2,1},{3,2},{4,3},{5,4},{6,5},{7,6},{8,7},{9,8},{10,9},{11,1... | collective-permute-start | bytes 138248 | tf_op jit(solution)/shard_map/ppermute | solution.py:16
  159.0 1.3 collective-permute-done.17
  160.8 1.9 collective-permute-start.18
  162.7 6.5 %collective-permute-start.19 = (f32[3,30,128]{2,1,0:T(8,128)S(1)}, f32[3,30,128]{2,1,0:T(8,128)S(1)}, u32[]{:S(2)}, u32[]{:S(2)}) collective-permute-start(f32[3,30,128]{2,1,0:T(8,128)S(1)} %pad_maximum_fusion.23), channel_id=1, source_target_pairs={{64,0},{128,64},{192,128},{256,192},{320,256},{384,320},{448,384},... | collective-permute-start | bytes 138248 | tf_op jit(solution)/shard_map/ppermute | solution.py:22
  169.4 1.6 collective-permute-done.19
  171.3 2.9 %gather_fusion.51 = f32[960,30]{1,0:T(8,128)S(1)} fusion(f32[30,1664]{0,1:T(8,128)S(1)} %copy.953, s32[1024]{0:T(1024)S(1)} %pad_clamp_fusion.11), kind=kCustom, calls=%fused_computation.31.clone | custom fusion | bytes 234240 | tf_op jit(solution)/shard_map/jit(_take)/gather | solution.py:31
  174.2 2.9 %gather_fusion.50 = f32[960,30]{1,0:T(8,128)S(1)} fusion(f32[30,1664]{0,1:T(8,128)S(1)} %copy.953, s32[1024]{0:T(1024)S(1)} %copy-done.8), kind=kCustom, calls=%fused_computation.30.clone | custom fusion | bytes 234240 | tf_op jit(solution)/shard_map/jit(_take)/gather | solution.py:31
  187.6 2.4 %collective-permute-start.20 = (f32[3,30,128]{1,2,0:T(8,128)S(1)}, f32[3,30,128]{1,2,0:T(8,128)S(1)}, u32[]{:S(2)}, u32[]{:S(2)}) collective-permute-start(f32[3,30,128]{1,2,0:T(8,128)S(1)} %pad_maximum_fusion.8), channel_id=1, source_target_pairs={{1,0},{2,1},{3,2},{4,3},{5,4},{6,5},{7,6},{8,7},{9,8},{10,9},{11,1... | collective-permute-start | bytes 138248 | tf_op jit(solution)/shard_map/ppermute | solution.py:16
  191.9 1.3 collective-permute-done.20
  193.2 1.9 collective-permute-start.22
  195.2 6.4 %collective-permute-start.23 = (f32[3,30,128]{1,2,0:T(8,128)S(1)}, f32[3,30,128]{1,2,0:T(8,128)S(1)}, u32[]{:S(2)}, u32[]{:S(2)}) collective-permute-start(f32[3,30,128]{1,2,0:T(8,128)S(1)} %pad_maximum_fusion.11), channel_id=1, source_target_pairs={{64,0},{128,64},{192,128},{256,192},{320,256},{384,320},{448,384},... | collective-permute-start | bytes 138248 | tf_op jit(solution)/shard_map/ppermute | solution.py:22
  201.6 1.7 collective-permute-done.22
  203.3 1.4 collective-permute-done.23
  204.8 1.7 gather_fusion.62
  206.5 1.7 gather_fusion.61
  208.1 1.7 gather_fusion.60
  (700 shorter events, 76.0 us)
Async XLA Ops:
  1.8 26.6 %copy-start.175 = (pred[128]{0:T(512)(128)(4,1)}, pred[128]{0:T(512)(128)(4,1)S(1)}, u32[]{:S(2)}) copy-start(pred[128]{0:T(512)(128)(4,1)S(1)} %get-tuple-element.343) | copy-start | bytes 388
  1.8 26.6 %copy-start.168 = (pred[128]{0:T(512)(128)(4,1)}, pred[128]{0:T(512)(128)(4,1)S(1)}, u32[]{:S(2)}) copy-start(pred[128]{0:T(512)(128)(4,1)S(1)} %get-tuple-element.283) | copy-start | bytes 388
  4.1 25.6 %collective-permute-start.1 = (f32[3,30,128]{2,1,0:T(8,128)S(1)}, f32[3,30,128]{2,1,0:T(8,128)S(1)}, u32[]{:S(2)}, u32[]{:S(2)}) collective-permute-start(f32[3,30,128]{2,1,0:T(8,128)S(1)} %pad_maximum_fusion.13), channel_id=1, source_target_pairs={{63,0},{0,1},{1,2},{2,3},{3,4},{4,5},{5,6},{6,7},{7,8},{8,9},{9,10... | collective-permute-start | bytes 138248 | tf_op jit(solution)/shard_map/ppermute | solution.py:16
  6.4 16.3 %copy-start = (f32[1,30,640]{2,0,1:T(1,128)S(1)}, f32[1,30,640]{2,0,1:T(1,128)}, u32[]{:S(2)}) copy-start(f32[1,30,640]{2,0,1:T(1,128)} %param.18) | copy-start | bytes 230404
  6.5 23.3 %collective-permute-start = (f32[3,30,128]{2,1,0:T(8,128)S(1)}, f32[3,30,128]{2,1,0:T(8,128)S(1)}, u32[]{:S(2)}, u32[]{:S(2)}) collective-permute-start(f32[3,30,128]{2,1,0:T(8,128)S(1)} %pad_maximum_fusion.12), channel_id=1, source_target_pairs={{1,0},{2,1},{3,2},{4,3},{5,4},{6,5},{7,6},{8,7},{9,8},{10,9},{11,1... | collective-permute-start | bytes 138248 | tf_op jit(solution)/shard_map/ppermute | solution.py:16
  22.8 22.8 %copy-start.137 = (pred[960]{0:T(1024)(128)(4,1)}, pred[960]{0:T(1024)(128)(4,1)S(1)}, u32[]{:S(2)}) copy-start(pred[960]{0:T(1024)(128)(4,1)S(1)} %compare_and_fusion.3) | copy-start | bytes 2884
  23.5 22.1 %copy-start.140 = (pred[960]{0:T(1024)(128)(4,1)}, pred[960]{0:T(1024)(128)(4,1)S(1)}, u32[]{:S(2)}) copy-start(pred[960]{0:T(1024)(128)(4,1)S(1)} %compare_and_fusion.4) | copy-start | bytes 2884
  26.8 81.8 %copy-start.7 = (s32[1024]{0:T(1024)}, s32[1024]{0:T(1024)S(1)}, u32[]{:S(2)}) copy-start(s32[1024]{0:T(1024)S(1)} %pad_clamp_fusion.12) | copy-start | bytes 12292
  26.8 21.7 %copy-start.170 = (pred[128]{0:T(512)(128)(4,1)}, pred[128]{0:T(512)(128)(4,1)S(1)}, u32[]{:S(2)}) copy-start(pred[128]{0:T(512)(128)(4,1)S(1)} %get-tuple-element.337) | copy-start | bytes 388
  26.8 21.8 %copy-start.165 = (pred[128]{0:T(512)(128)(4,1)}, pred[128]{0:T(512)(128)(4,1)S(1)}, u32[]{:S(2)}) copy-start(pred[128]{0:T(512)(128)(4,1)S(1)} %get-tuple-element.325) | copy-start | bytes 388
  26.9 21.8 %copy-start.162 = (pred[128]{0:T(512)(128)(4,1)}, pred[128]{0:T(512)(128)(4,1)S(1)}, u32[]{:S(2)}) copy-start(pred[128]{0:T(512)(128)(4,1)S(1)} %get-tuple-element.327) | copy-start | bytes 388
  26.9 24.6 %copy-start.152 = (pred[128]{0:T(512)(128)(4,1)}, pred[128]{0:T(512)(128)(4,1)S(1)}, u32[]{:S(2)}) copy-start(pred[128]{0:T(512)(128)(4,1)S(1)} %get-tuple-element.331) | copy-start | bytes 388
  26.9 24.7 %copy-start.149 = (pred[128]{0:T(512)(128)(4,1)}, pred[128]{0:T(512)(128)(4,1)S(1)}, u32[]{:S(2)}) copy-start(pred[128]{0:T(512)(128)(4,1)S(1)} %get-tuple-element.333) | copy-start | bytes 388
  26.9 24.8 %copy-start.146 = (pred[128]{0:T(512)(128)(4,1)}, pred[128]{0:T(512)(128)(4,1)S(1)}, u32[]{:S(2)}) copy-start(pred[128]{0:T(512)(128)(4,1)S(1)} %get-tuple-element.335) | copy-start | bytes 388
  26.9 28.5 %copy-start.155 = (pred[128]{0:T(512)(128)(4,1)}, pred[128]{0:T(512)(128)(4,1)S(1)}, u32[]{:S(2)}) copy-start(pred[128]{0:T(512)(128)(4,1)S(1)} %get-tuple-element.329) | copy-start | bytes 388
  26.9 28.6 %copy-start.143 = (pred[128]{0:T(512)(128)(4,1)}, pred[128]{0:T(512)(128)(4,1)S(1)}, u32[]{:S(2)}) copy-start(pred[128]{0:T(512)(128)(4,1)S(1)} %get-tuple-element.265) | copy-start | bytes 388
  26.9 19.6 %copy-start.184 = (s32[1024]{0:T(1024)}, s32[1024]{0:T(1024)S(1)}, u32[]{:S(2)}) copy-start(s32[1024]{0:T(1024)S(1)} %pad_clamp_fusion.4) | copy-start | bytes 12292
  26.9 20.2 %copy-start.185 = (s32[1024]{0:T(1024)}, s32[1024]{0:T(1024)S(1)}, u32[]{:S(2)}) copy-start(s32[1024]{0:T(1024)S(1)} %pad_clamp_fusion.5) | copy-start | bytes 12292
  27.0 20.9 %copy-start.186 = (s32[1024]{0:T(1024)}, s32[1024]{0:T(1024)S(1)}, u32[]{:S(2)}) copy-start(s32[1024]{0:T(1024)S(1)} %pad_clamp_fusion.6) | copy-start | bytes 12292
  27.0 21.9 %copy-start.187 = (s32[1024]{0:T(1024)}, s32[1024]{0:T(1024)S(1)}, u32[]{:S(2)}) copy-start(s32[1024]{0:T(1024)S(1)} %pad_clamp_fusion.7) | copy-start | bytes 12292
  27.0 22.5 %copy-start.188 = (s32[1024]{0:T(1024)}, s32[1024]{0:T(1024)S(1)}, u32[]{:S(2)}) copy-start(s32[1024]{0:T(1024)S(1)} %pad_clamp_fusion.8) | copy-start | bytes 12292
  27.0 23.1 %copy-start.189 = (s32[1024]{0:T(1024)}, s32[1024]{0:T(1024)S(1)}, u32[]{:S(2)}) copy-start(s32[1024]{0:T(1024)S(1)} %pad_clamp_fusion.9) | copy-start | bytes 12292
  27.1 23.7 %copy-start.190 = (s32[1024]{0:T(1024)}, s32[1024]{0:T(1024)S(1)}, u32[]{:S(2)}) copy-start(s32[1024]{0:T(1024)S(1)} %pad_clamp_fusion.10) | copy-start | bytes 12292
  27.1 27.6 %copy-start.191 = (s32[1024]{0:T(1024)}, s32[1024]{0:T(1024)S(1)}, u32[]{:S(2)}) copy-start(s32[1024]{0:T(1024)S(1)} %pad_clamp_fusion.3) | copy-start | bytes 12292
  27.8 113.0 %copy-start.3 = (s32[1024]{0:T(1024)}, s32[1024]{0:T(1024)S(1)}, u32[]{:S(2)}) copy-start(s32[1024]{0:T(1024)S(1)} %pad_clamp_fusion.1) | copy-start | bytes 12292
  28.5 114.0 %copy-start.5 = (s32[1024]{0:T(1024)}, s32[1024]{0:T(1024)S(1)}, u32[]{:S(2)}) copy-start(s32[1024]{0:T(1024)S(1)} %pad_clamp_fusion.2) | copy-start | bytes 12292
  29.8 8.1 %collective-permute-start.2 = (f32[3,30,128]{2,1,0:T(8,128)S(1)}, f32[3,30,128]{2,1,0:T(8,128)S(1)}, u32[]{:S(2)}, u32[]{:S(2)}) collective-permute-start(f32[3,30,128]{2,1,0:T(8,128)S(1)} %pad_maximum_fusion.14), channel_id=1, source_target_pairs={{0,64},{64,128},{128,192},{192,256},{256,320},{320,384},{384,448},... | collective-permute-start | bytes 138248 | tf_op jit(solution)/shard_map/ppermute | solution.py:22
  33.3 6.2 %collective-permute-start.3 = (f32[3,30,128]{2,1,0:T(8,128)S(1)}, f32[3,30,128]{2,1,0:T(8,128)S(1)}, u32[]{:S(2)}, u32[]{:S(2)}) collective-permute-start(f32[3,30,128]{2,1,0:T(8,128)S(1)} %pad_maximum_fusion.15), channel_id=1, source_target_pairs={{64,0},{128,64},{192,128},{256,192},{320,256},{384,320},{448,384},... | collective-permute-start | bytes 138248 | tf_op jit(solution)/shard_map/ppermute | solution.py:22
  48.8 6.8 %collective-permute-start.5 = (f32[3,30,128]{1,2,0:T(8,128)S(1)}, f32[3,30,128]{1,2,0:T(8,128)S(1)}, u32[]{:S(2)}, u32[]{:S(2)}) collective-permute-start(f32[3,30,128]{1,2,0:T(8,128)S(1)} %pad_maximum_fusion.1), channel_id=1, source_target_pairs={{63,0},{0,1},{1,2},{2,3},{3,4},{4,5},{5,6},{6,7},{7,8},{8,9},{9,10... | collective-permute-start | bytes 138248 | tf_op jit(solution)/shard_map/ppermute | solution.py:16
  51.8 6.1 %collective-permute-start.4 = (f32[3,30,128]{1,2,0:T(8,128)S(1)}, f32[3,30,128]{1,2,0:T(8,128)S(1)}, u32[]{:S(2)}, u32[]{:S(2)}) collective-permute-start(f32[3,30,128]{1,2,0:T(8,128)S(1)} %pad_maximum_fusion), channel_id=1, source_target_pairs={{1,0},{2,1},{3,2},{4,3},{5,4},{6,5},{7,6},{8,7},{9,8},{10,9},{11,1... | collective-permute-start | bytes 138248 | tf_op jit(solution)/shard_map/ppermute | solution.py:16
  58.0 10.0 %collective-permute-start.6 = (f32[3,30,128]{1,2,0:T(8,128)S(1)}, f32[3,30,128]{1,2,0:T(8,128)S(1)}, u32[]{:S(2)}, u32[]{:S(2)}) collective-permute-start(f32[3,30,128]{1,2,0:T(8,128)S(1)} %pad_maximum_fusion.2), channel_id=1, source_target_pairs={{0,64},{64,128},{128,192},{192,256},{256,320},{320,384},{384,448},... | collective-permute-start | bytes 138248 | tf_op jit(solution)/shard_map/ppermute | solution.py:22
  61.3 8.2 %collective-permute-start.7 = (f32[3,30,128]{1,2,0:T(8,128)S(1)}, f32[3,30,128]{1,2,0:T(8,128)S(1)}, u32[]{:S(2)}, u32[]{:S(2)}) collective-permute-start(f32[3,30,128]{1,2,0:T(8,128)S(1)} %pad_maximum_fusion.3), channel_id=1, source_target_pairs={{64,0},{128,64},{192,128},{256,192},{320,256},{384,320},{448,384},... | collective-permute-start | bytes 138248 | tf_op jit(solution)/shard_map/ppermute | solution.py:22
  87.6 6.1 %collective-permute-start.9 = (f32[3,30,128]{2,1,0:T(8,128)S(1)}, f32[3,30,128]{2,1,0:T(8,128)S(1)}, u32[]{:S(2)}, u32[]{:S(2)}) collective-permute-start(f32[3,30,128]{2,1,0:T(8,128)S(1)} %pad_maximum_fusion.17), channel_id=1, source_target_pairs={{63,0},{0,1},{1,2},{2,3},{3,4},{4,5},{5,6},{6,7},{7,8},{8,9},{9,10... | collective-permute-start | bytes 138248 | tf_op jit(solution)/shard_map/ppermute | solution.py:16
  90.8 4.7 %collective-permute-start.8 = (f32[3,30,128]{2,1,0:T(8,128)S(1)}, f32[3,30,128]{2,1,0:T(8,128)S(1)}, u32[]{:S(2)}, u32[]{:S(2)}) collective-permute-start(f32[3,30,128]{2,1,0:T(8,128)S(1)} %pad_maximum_fusion.16), channel_id=1, source_target_pairs={{1,0},{2,1},{3,2},{4,3},{5,4},{6,5},{7,6},{8,7},{9,8},{10,9},{11,1... | collective-permute-start | bytes 138248 | tf_op jit(solution)/shard_map/ppermute | solution.py:16
  95.4 8.3 %collective-permute-start.10 = (f32[3,30,128]{2,1,0:T(8,128)S(1)}, f32[3,30,128]{2,1,0:T(8,128)S(1)}, u32[]{:S(2)}, u32[]{:S(2)}) collective-permute-start(f32[3,30,128]{2,1,0:T(8,128)S(1)} %pad_maximum_fusion.18), channel_id=1, source_target_pairs={{0,64},{64,128},{128,192},{192,256},{256,320},{320,384},{384,448},... | collective-permute-start | bytes 138248 | tf_op jit(solution)/shard_map/ppermute | solution.py:22
  97.7 7.6 %collective-permute-start.11 = (f32[3,30,128]{2,1,0:T(8,128)S(1)}, f32[3,30,128]{2,1,0:T(8,128)S(1)}, u32[]{:S(2)}, u32[]{:S(2)}) collective-permute-start(f32[3,30,128]{2,1,0:T(8,128)S(1)} %pad_maximum_fusion.19), channel_id=1, source_target_pairs={{64,0},{128,64},{192,128},{256,192},{320,256},{384,320},{448,384},... | collective-permute-start | bytes 138248 | tf_op jit(solution)/shard_map/ppermute | solution.py:22
  119.9 6.3 %collective-permute-start.13 = (f32[3,30,128]{1,2,0:T(8,128)S(1)}, f32[3,30,128]{1,2,0:T(8,128)S(1)}, u32[]{:S(2)}, u32[]{:S(2)}) collective-permute-start(f32[3,30,128]{1,2,0:T(8,128)S(1)} %pad_maximum_fusion.5), channel_id=1, source_target_pairs={{63,0},{0,1},{1,2},{2,3},{3,4},{4,5},{5,6},{6,7},{7,8},{8,9},{9,10... | collective-permute-start | bytes 138248 | tf_op jit(solution)/shard_map/ppermute | solution.py:16
  121.9 5.6 %collective-permute-start.12 = (f32[3,30,128]{1,2,0:T(8,128)S(1)}, f32[3,30,128]{1,2,0:T(8,128)S(1)}, u32[]{:S(2)}, u32[]{:S(2)}) collective-permute-start(f32[3,30,128]{1,2,0:T(8,128)S(1)} %pad_maximum_fusion.4), channel_id=1, source_target_pairs={{1,0},{2,1},{3,2},{4,3},{5,4},{6,5},{7,6},{8,7},{9,8},{10,9},{11,1... | collective-permute-start | bytes 138248 | tf_op jit(solution)/shard_map/ppermute | solution.py:16
  127.6 10.0 %collective-permute-start.14 = (f32[3,30,128]{1,2,0:T(8,128)S(1)}, f32[3,30,128]{1,2,0:T(8,128)S(1)}, u32[]{:S(2)}, u32[]{:S(2)}) collective-permute-start(f32[3,30,128]{1,2,0:T(8,128)S(1)} %pad_maximum_fusion.6), channel_id=1, source_target_pairs={{0,64},{64,128},{128,192},{192,256},{256,320},{320,384},{384,448},... | collective-permute-start | bytes 138248 | tf_op jit(solution)/shard_map/ppermute | solution.py:22
  129.5 9.5 %collective-permute-start.15 = (f32[3,30,128]{1,2,0:T(8,128)S(1)}, f32[3,30,128]{1,2,0:T(8,128)S(1)}, u32[]{:S(2)}, u32[]{:S(2)}) collective-permute-start(f32[3,30,128]{1,2,0:T(8,128)S(1)} %pad_maximum_fusion.7), channel_id=1, source_target_pairs={{64,0},{128,64},{192,128},{256,192},{320,256},{384,320},{448,384},... | collective-permute-start | bytes 138248 | tf_op jit(solution)/shard_map/ppermute | solution.py:22
  155.6 4.7 %collective-permute-start.17 = (f32[3,30,128]{2,1,0:T(8,128)S(1)}, f32[3,30,128]{2,1,0:T(8,128)S(1)}, u32[]{:S(2)}, u32[]{:S(2)}) collective-permute-start(f32[3,30,128]{2,1,0:T(8,128)S(1)} %pad_maximum_fusion.21), channel_id=1, source_target_pairs={{63,0},{0,1},{1,2},{2,3},{3,4},{4,5},{5,6},{6,7},{7,8},{8,9},{9,10... | collective-permute-start | bytes 138248 | tf_op jit(solution)/shard_map/ppermute | solution.py:16
  156.1 4.7 %collective-permute-start.16 = (f32[3,30,128]{2,1,0:T(8,128)S(1)}, f32[3,30,128]{2,1,0:T(8,128)S(1)}, u32[]{:S(2)}, u32[]{:S(2)}) collective-permute-start(f32[3,30,128]{2,1,0:T(8,128)S(1)} %pad_maximum_fusion.20), channel_id=1, source_target_pairs={{1,0},{2,1},{3,2},{4,3},{5,4},{6,5},{7,6},{8,7},{9,8},{10,9},{11,1... | collective-permute-start | bytes 138248 | tf_op jit(solution)/shard_map/ppermute | solution.py:16
  160.8 8.6 %collective-permute-start.18 = (f32[3,30,128]{2,1,0:T(8,128)S(1)}, f32[3,30,128]{2,1,0:T(8,128)S(1)}, u32[]{:S(2)}, u32[]{:S(2)}) collective-permute-start(f32[3,30,128]{2,1,0:T(8,128)S(1)} %pad_maximum_fusion.22), channel_id=1, source_target_pairs={{0,64},{64,128},{128,192},{192,256},{256,320},{320,384},{384,448},... | collective-permute-start | bytes 138248 | tf_op jit(solution)/shard_map/ppermute | solution.py:22
  162.7 8.2 %collective-permute-start.19 = (f32[3,30,128]{2,1,0:T(8,128)S(1)}, f32[3,30,128]{2,1,0:T(8,128)S(1)}, u32[]{:S(2)}, u32[]{:S(2)}) collective-permute-start(f32[3,30,128]{2,1,0:T(8,128)S(1)} %pad_maximum_fusion.23), channel_id=1, source_target_pairs={{64,0},{128,64},{192,128},{256,192},{320,256},{384,320},{448,384},... | collective-permute-start | bytes 138248 | tf_op jit(solution)/shard_map/ppermute | solution.py:22
  185.5 6.3 %collective-permute-start.21 = (f32[3,30,128]{1,2,0:T(8,128)S(1)}, f32[3,30,128]{1,2,0:T(8,128)S(1)}, u32[]{:S(2)}, u32[]{:S(2)}) collective-permute-start(f32[3,30,128]{1,2,0:T(8,128)S(1)} %pad_maximum_fusion.9), channel_id=1, source_target_pairs={{63,0},{0,1},{1,2},{2,3},{3,4},{4,5},{5,6},{6,7},{7,8},{8,9},{9,10... | collective-permute-start | bytes 138248 | tf_op jit(solution)/shard_map/ppermute | solution.py:16
  187.6 5.6 %collective-permute-start.20 = (f32[3,30,128]{1,2,0:T(8,128)S(1)}, f32[3,30,128]{1,2,0:T(8,128)S(1)}, u32[]{:S(2)}, u32[]{:S(2)}) collective-permute-start(f32[3,30,128]{1,2,0:T(8,128)S(1)} %pad_maximum_fusion.8), channel_id=1, source_target_pairs={{1,0},{2,1},{3,2},{4,3},{5,4},{6,5},{7,6},{8,7},{9,8},{10,9},{11,1... | collective-permute-start | bytes 138248 | tf_op jit(solution)/shard_map/ppermute | solution.py:16
  193.2 10.0 %collective-permute-start.22 = (f32[3,30,128]{1,2,0:T(8,128)S(1)}, f32[3,30,128]{1,2,0:T(8,128)S(1)}, u32[]{:S(2)}, u32[]{:S(2)}) collective-permute-start(f32[3,30,128]{1,2,0:T(8,128)S(1)} %pad_maximum_fusion.10), channel_id=1, source_target_pairs={{0,64},{64,128},{128,192},{192,256},{256,320},{320,384},{384,448},... | collective-permute-start | bytes 138248 | tf_op jit(solution)/shard_map/ppermute | solution.py:22
  195.2 9.5 %collective-permute-start.23 = (f32[3,30,128]{1,2,0:T(8,128)S(1)}, f32[3,30,128]{1,2,0:T(8,128)S(1)}, u32[]{:S(2)}, u32[]{:S(2)}) collective-permute-start(f32[3,30,128]{1,2,0:T(8,128)S(1)} %pad_maximum_fusion.11), channel_id=1, source_target_pairs={{64,0},{128,64},{192,128},{256,192},{320,256},{384,320},{448,384},... | collective-permute-start | bytes 138248 | tf_op jit(solution)/shard_map/ppermute | solution.py:22
  (181 other events, 235.1 us)
where the time goes:
time: 219 us; the launch traced here: 215 us
  local copies, waits for them, and re-layouts  92.6 us (42%)
  starting transfers between devices  79.5 us (36%)
  waiting for transfers between devices  25.4 us (12%)
  other arithmetic  13.8 us (6%)
  between operations  4.22 us (2%)
    ppermute x12, starting transfers between devices, passed_along(): lax.ppermute(value, axis, [(source, source + steps) for source in range(f...  49.5 us
    gather x72, local copies, waits for them, and re-layouts, extend(): jnp.take(source, send_list[member], axis=1)  36.5 us
    ppermute x12, starting transfers between devices, from_behind(): return lax.ppermute(block, axis, route)  30 us
    unnamed x459, local copies, waits for them, and re-layouts  20 us
    ppermute x12, waiting for transfers between devices, passed_along(): lax.ppermute(value, axis, [(source, source + steps) for source in range(f...  14.2 us
    ppermute x12, waiting for transfers between devices, from_behind(): return lax.ppermute(block, axis, route)  11.1 us
    gather x3, local copies, waits for them, and re-layouts, edge_update(): jnp.take(extended, edge_cells[0], axis=1)  8.64 us
    gather x3, local copies, waits for them, and re-layouts, edge_update(): jnp.take(extended, edge_cells[1], axis=1)  8.64 us
  transfers between devices with their start and end apart: 24, of which 20 were waited for; matrix products, arithmetic and copies ran while one was open for 6% of the time, Pallas kernels for 0%

commit v1 on v0

v1 whole, which is shorter than its diff:
```python
import functools

import jax
import jax.numpy as jnp
from jax import lax
from jax.experimental import pallas as pl
from jax.experimental.pallas import tpu as pltpu
from jax.sharding import PartitionSpec as P

NSUB = 3
C = 640
E = 960
EP = 1024
H = 128
L = 30
LP = 32
N = 8 * H
DIRECTIONS = ((-1, -1), (-1, 0), (-1, 1), (0, -1), (0, 1), (1, -1), (1, 0), (1, 1))
ORDER = (0, 2, 5, 7, 1, 6, 3, 4)
F32, BF16 = jnp.float32, jnp.bfloat16
MESH = pl.DeviceIdType.MESH


def split(x):
    high = x.astype(BF16)
    return high, (x - high.astype(F32)).astype(BF16)


def dot(a, b):
    return jnp.dot(a, b, preferred_element_type=F32)


def halves(x):
    return x[:LP] + x[LP:]


def kernel(
    n_lat, n_lon,
    p_hbm, v_hbm, ec_hbm, ce_hbm, sc_hbm, se_hbm, inv_hbm, w_hbm, ss_hbm, cp_hbm,
    p_out, v_out,
    p_in, v_in, ec_in, ce_in, sc_in, se_in, inv_in, w_in, ss_in, cp_in,
    pres, vel, pieces_out, pieces_in,
    pres_hl, vel_hl, pick_c, pick_e, diff, diff_l, weight,
    rows_l, grad_l, vel_l, right, solve_in, solve_mid, coef_a, coef_b, coef_r,
    in_sem, out_sem, send_sem, recv_sem,
):
    a, b = lax.axis_index("lat"), lax.axis_index("lon")
    not_first, not_last = a > 0, a < n_lat - 1

    def neighbour(member):
        p, q = DIRECTIONS[member]
        return (a + p, lax.rem(b + q + n_lon, n_lon))

    barrier = pltpu.get_barrier_semaphore()

    def greet(members):
        for member in members:
            pl.semaphore_signal(barrier, inc=1, device_id=neighbour(member), device_id_type=MESH)

    greet((3, 4))
    pl.when(not_first)(lambda: greet((0, 1, 2)))
    pl.when(not_last)(lambda: greet((5, 6, 7)))

    sources = (sc_hbm, p_hbm, se_hbm, v_hbm, ec_hbm, inv_hbm, ce_hbm, w_hbm, ss_hbm, cp_hbm)
    targets = (sc_in, p_in, se_in, v_in, ec_in, inv_in, ce_in, w_in, ss_in, cp_in)
    loads = []
    for i, (source, target) in enumerate(zip(sources, targets)):
        view = source if source.ndim == 2 else source.at[0]
        loads.append(pltpu.make_async_copy(view, target, in_sem.at[i]))
        loads[-1].start()

    def copy(exchange, member):
        return pltpu.make_async_remote_copy(
            src_ref=pieces_out.at[exchange, member],
            dst_ref=pieces_in.at[exchange, 7 - member],
            send_sem=send_sem.at[exchange, member],
            recv_sem=recv_sem.at[exchange, 7 - member],
            device_id=neighbour(member),
            device_id_type=MESH,
        )

    def by_row(members, action):
        for member in members:
            row = DIRECTIONS[member][0]
            if row == 0:
                action(member)
            else:
                pl.when(not_first if row < 0 else not_last)(functools.partial(action, member))

    def receive(exchange, members, target, base):
        for member in members:
            pltpu.make_async_remote_copy(
                src_ref=pieces_out.at[exchange, member],
                dst_ref=pieces_in.at[exchange, member],
                send_sem=send_sem.at[exchange, member],
                recv_sem=recv_sem.at[exchange, member],
                device_id=neighbour(member),
                device_id_type=MESH,
            ).wait_recv()
        for member in members:
            high, low = split(pieces_in[exchange, member])
            target[:LP, base + member * H:base + (member + 1) * H] = high
            target[LP:, base + member * H:base + (member + 1) * H] = low

    def receive_rest(exchange, target, base):
        pl.when(not_first)(lambda: receive(exchange, (0, 1, 2), target, base))
        pl.when(not_last)(lambda: receive(exchange, (5, 6, 7), target, base))

    def one_hot_rows(start, count, width):
        return (lax.broadcasted_iota(jnp.int32, (count, width), 0) + start).astype(F32)

    def build_pick(lists_ref, target, own):
        lists = lists_ref[...].astype(F32)
        picks = jnp.concatenate([lists[member:member + 1] for member in ORDER], axis=1)

        def step(i, carry):
            start = pl.multiple_of(i * 32, 32)
            hit = one_hot_rows(start, 32, N) == picks
            target[pl.ds(start, 32), :] = jnp.where(hit, 1.0, 0.0).astype(BF16)
            return carry

        lax.fori_loop(0, own // 32, step, 0)

    def build_diff(first, second, target):
        def step(i, carry):
            start = pl.multiple_of(i * 32, 32)
            rows = one_hot_rows(start, 32, N)
            hit = jnp.where(rows == second, 1.0, 0.0) - jnp.where(rows == first, 1.0, 0.0)
            target[pl.ds(start, 32), :] = hit.astype(BF16)
            return carry

        lax.fori_loop(0, (C + N) // 32, step, 0)

    def build_weight():
        places = ce_in[...].astype(F32)
        places = jnp.where(places >= E, places + (EP - E), places)
        weights = w_in[...] * ss_in[...]

        def step(i, carry):
            start = pl.multiple_of(i * 32, 32)
            rows = one_hot_rows(start, 32, C)
            total = jnp.where(rows == places[0:1], weights[0:1], 0.0)
            total = total + jnp.where(rows == places[1:2], weights[1:2], 0.0)
            total = total + jnp.where(rows == places[2:3], weights[2:3], 0.0)
            high, low = split(total)
            weight[pl.ds(start, 32), :C] = high
            weight[pl.ds(start, 32), C:] = low
            return carry

        lax.fori_loop(0, (EP + N) // 32, step, 0)

    def to_columns(x, target):
        for block in range(C // H):
            target[pl.ds(block, LP, stride=8), :] = x[:, block * H:(block + 1) * H]

    def build_solver():
        coupling = jnp.concatenate([cp_in[...], jnp.zeros((LP - L, C), F32)], axis=0)
        to_columns(coupling, solve_in)
        below, inverse = None, None
        for k in range(L):
            here = solve_in[8 * k:8 * k + 8, :]
            divisor = 1.0 + here
            if k > 0:
                divisor = divisor + below - below * (below * inverse)
            inverse = 1.0 / divisor
            coef_a[8 * k:8 * k + 8, :] = inverse
            if k > 0:
                coef_b[8 * k:8 * k + 8, :] = below * inverse
            coef_r[8 * k:8 * k + 8, :] = here * inverse
            below = here

    def solve():
        current = solve_in[0:8, :] * coef_a[0:8, :]
        solve_mid[0:8, :] = current
        for k in range(1, L):
            rows = slice(8 * k, 8 * k + 8)
            current = solve_in[rows, :] * coef_a[rows, :] + coef_b[rows, :] * current
            solve_mid[rows, :] = current
        for k in range(L - 2, -1, -1):
            rows = slice(8 * k, 8 * k + 8)
            current = solve_mid[rows, :] + coef_r[rows, :] * current
            solve_mid[rows, :] = current
        for block in range(C // H):
            x = solve_mid[pl.ds(block, LP, stride=8), :]
            pres[:, block * H:(block + 1) * H] = x
            high, low = split(x)
            pres_hl[:LP, block * H:(block + 1) * H] = high
            pres_hl[LP:, block * H:(block + 1) * H] = low

    def pressure_pieces(exchange):
        for chunk in range(4):
            cols = slice(chunk * 256, chunk * 256 + 256)
            picked = halves(dot(pres_hl[:, :C], pick_c[:, cols]))
            for half in range(2):
                pieces_out[exchange, ORDER[2 * chunk + half]] = picked[:, half * H:(half + 1) * H]

    def own_gradient():
        for chunk in range(4):
            cols = slice(chunk * 256, chunk * 256 + 256)
            grad_l[:, cols] = halves(dot(pres_hl[:, :C], diff_l[:C, cols]))

    loads[0].wait()
    build_pick(sc_in, pick_c, C)
    loads[1].wait()
    start = jnp.concatenate([p_in[...], jnp.zeros((LP - L, C), F32)], axis=0)
    pres[...] = start
    high, low = split(start)
    pres_hl[:LP, :C] = high
    pres_hl[LP:, :C] = low
    pres_hl[:, C:] = jnp.zeros((2 * LP, N), BF16)
    pressure_pieces(0)
    pl.semaphore_wait(barrier, 2 + 3 * lax.min(a, 1) + 3 * lax.min(n_lat - 1 - a, 1))
    by_row(ORDER, lambda member: copy(0, member).start())

    loads[2].wait()
    build_pick(se_in, pick_e, EP)
    for i in range(3, 10):
        loads[i].wait()
    vel[...] = jnp.zeros_like(vel)
    vel[:L, :E] = v_in[...]
    high, low = split(vel[...])
    vel_hl[:LP, :EP] = high
    vel_hl[LP:, :EP] = low
    vel_hl[:, EP:] = jnp.zeros((2 * LP, N), BF16)
    rows_l[...] = jnp.full(rows_l.shape, -1.0, F32)
    rows_l[0:2, :E] = ec_in[...].astype(F32)
    rows_l[2:3, :] = jnp.zeros((1, EP), F32)
    rows_l[2:3, :E] = 0.5 * inv_in[...]
    own_rows = rows_l[...]
    cells_first, cells_second, factor = own_rows[0:1], own_rows[1:2], own_rows[2:3]
    coarse = jnp.floor(own_rows[0:2] * (1.0 / H))
    fine = own_rows[0:2] - H * coarse
    factor_high = factor.astype(BF16).astype(F32)
    factor_mid = (factor - factor_high).astype(BF16).astype(F32)
    factor_low = factor - factor_high - factor_mid
    parts = jnp.concatenate(
        [coarse, fine, factor_high, factor_mid, factor_low, jnp.zeros((9, EP), F32)], axis=0
    ).astype(BF16)
    for chunk in range(4):
        cols = slice(chunk * 256, chunk * 256 + 256)
        vel_l[:, cols] = halves(dot(vel_hl[:, :EP], pick_e[:, cols]))
        found = dot(parts, pick_e[:, cols])
        rows_l[4:6, cols] = found[0:2] * H + found[2:4]
        rows_l[6:7, cols] = found[4:5] + found[5:6] + found[6:7]
    sent_rows = rows_l[...]
    build_diff(sent_rows[4:5], sent_rows[5:6], diff_l)
    own_gradient()
    build_diff(cells_first, cells_second, diff)

    def substep(s, carry):
        first, second = 2 * s, 2 * s + 1
        receive(first, (3, 4), pres_hl, C)
        near = slice(C + 3 * H, C + 5 * H)
        for chunk in range(4):
            cols = slice(chunk * 256, chunk * 256 + 256)
            grad_l[:, cols] = grad_l[:, cols] + halves(dot(pres_hl[:, near], diff_l[near, cols]))
        receive_rest(first, pres_hl, C)
        behind, ahead = slice(C, C + 3 * H), slice(C + 5 * H, C + 8 * H)
        for chunk in range(4):
            cols = slice(chunk * 256, chunk * 256 + 256)
            far = dot(pres_hl[:, behind], diff_l[behind, cols])
            far = far + dot(pres_hl[:, ahead], diff_l[ahead, cols])
            moved = vel_l[:, cols] - rows_l[6:7, cols] * (grad_l[:, cols] + halves(far))
            vel_l[:, cols] = moved
            for half in range(2):
                pieces_out[second, ORDER[2 * chunk + half]] = moved[:, half * H:(half + 1) * H]
            by_row(ORDER[2 * chunk:2 * chunk + 2], lambda member: copy(second, member).start())

        for chunk in range(4):
            cols = slice(chunk * 256, chunk * 256 + 256)
            gradient = halves(dot(pres_hl[...], diff[:, cols]))
            moved = vel[:, cols] - rows_l[2:3, cols] * gradient
            vel[:, cols] = moved
            high, low = split(moved)
            vel_hl[:LP, cols] = high
            vel_hl[LP:, cols] = low

        @pl.when(s == 0)
        def _():
            build_weight()
            build_solver()

        @pl.when(s == NSUB - 1)
        def _():
            v_in[...] = vel[:L, :E]
            pltpu.make_async_copy(v_in, v_out.at[0], out_sem.at[0]).start()

        def divergence(places):
            wide = dot(vel_hl[:, places], weight[places, :])
            return halves(wide[:, :C] + wide[:, C:])

        right[...] = pres[...] - divergence(slice(0, EP))
        receive(second, (3, 4), vel_hl, EP)
        right[...] = right[...] - divergence(slice(EP + 3 * H, EP + 5 * H))
        receive_rest(second, vel_hl, EP)
        total = divergence(slice(EP, EP + 3 * H)) + divergence(slice(EP + 5 * H, EP + 8 * H))
        to_columns(right[...] - total, solve_in)
        solve()

        @pl.when(s < NSUB - 1)
        def _():
            pressure_pieces(second + 1)
            by_row(ORDER, lambda member: copy(second + 1, member).start())
            own_gradient()

        return carry

    lax.fori_loop(0, NSUB, substep, 0)
    p_in[...] = pres[:L, :]
    pressure_store = pltpu.make_async_copy(p_in, p_out.at[0], out_sem.at[1])
    pressure_store.start()
    for exchange in range(2 * NSUB):
        by_row(ORDER, lambda member: copy(exchange, member).wait_send())
    pltpu.make_async_copy(v_in, v_out.at[0], out_sem.at[0]).wait()
    pressure_store.wait()


def solution(mesh):
    n_lat, n_lon = mesh.shape["lat"], mesh.shape["lon"]
    any_space = pl.BlockSpec(memory_space=pl.ANY)
    vmem = pltpu.VMEM
    i32 = jnp.int32

    def on_device(*operands):
        return pl.pallas_call(
            functools.partial(kernel, n_lat, n_lon),
            out_shape=(
                jax.ShapeDtypeStruct((1, L, C), F32),
                jax.ShapeDtypeStruct((1, L, E), F32),
            ),
            in_specs=[any_space] * 10,
            out_specs=(any_space, any_space),
            scratch_shapes=[
                vmem((L, C), F32), vmem((L, E), F32),
                vmem((2, E), i32), vmem((3, C), i32), vmem((8, H), i32), vmem((8, H), i32),
                vmem((1, E), F32), vmem((3, C), F32), vmem((1, C), F32), vmem((L, C), F32),
                vmem((LP, C), F32), vmem((LP, EP), F32),
                vmem((2 * NSUB, 8, LP, H), F32), vmem((2 * NSUB, 8, LP, H), F32),
                vmem((2 * LP, C + N), BF16), vmem((2 * LP, EP + N), BF16),
                vmem((C, N), BF16), vmem((EP, N), BF16),
                vmem((C + N, N), BF16), vmem((C + N, N), BF16), vmem((EP + N, 2 * C), BF16),
                vmem((8, N), F32), vmem((LP, N), F32), vmem((LP, N), F32), vmem((LP, C), F32),
                vmem((8 * LP, H), F32), vmem((8 * LP, H), F32),
                vmem((8 * LP, H), F32), vmem((8 * LP, H), F32), vmem((8 * LP, H), F32),
                pltpu.SemaphoreType.DMA((10,)), pltpu.SemaphoreType.DMA((2,)),
                pltpu.SemaphoreType.DMA((2 * NSUB, 8)), pltpu.SemaphoreType.DMA((2 * NSUB, 8)),
            ],
            compiler_params=pltpu.CompilerParams(
                collective_id=0, has_side_effects=True, vmem_limit_bytes=60 * 1024 * 1024
            ),
        )(*operands)

    spec3, spec2 = P("lat", None, "lon"), P("lat", "lon")
    return jax.shard_map(
        on_device,
        mesh=mesh,
        in_specs=(spec3, spec3, spec3, spec3, spec3, spec3, spec2, spec3, spec2, spec3),
        out_specs=(spec3, spec3),
        check_vma=False,
    )
```

time: 219 us -> 61.4 us (0.28); the launches traced: 215 us -> 61.2 us
  local copies, waits for them, and re-layouts: 92.6 us -> 7.19 us
  starting transfers between devices: 79.5 us -> 0 us
  Pallas kernels: 0 us -> 53.3 us
  waiting for transfers between devices: 25.4 us -> 0 us
  other arithmetic: 13.8 us -> 0 us
  between operations: 4.22 us -> 0.66 us
    ppermute x24 -> x0, starting transfers between devices: 79.5 us -> none  [the longest x12 49.5 us: passed_along(): lax.ppermute(value, axis, [(source, source + steps) for source in range(f...]
    gather x96 -> x0, local copies, waits for them, and re-layouts: 70.1 us -> none  [the longest x72 36.5 us: extend(): jnp.take(source, send_list[member], axis=1)]
    pallas_call x0 -> x1, Pallas kernels: none -> 53.3 us  [on_device(): pl.pallas_call(functools.partial(kernel, n_lat, n_lon), out_shape=(jax.Sh...]
    ppermute x24 -> x0, waiting for transfers between devices: 25.4 us -> none  [the longest x12 14.2 us: passed_along(): lax.ppermute(value, axis, [(source, source + steps) for source in range(f...]
    unnamed x459 -> x13, local copies, waits for them, and re-layouts: 20 us -> 4.78 us
    sub x6 -> x0, other arithmetic: 3.21 us -> none  [the longest x3 2.42 us: column_solve(): result.insert(0, scaled[level_index] - ratios[level_index] * result[0])]
    unnamed x4 -> x0, other arithmetic: 3.21 us -> none
    div x3 -> x0, other arithmetic: 3.01 us -> none  [column_solve(): current = (right_side[level_index] - lower_term * scaled[-1]) / divisor]
  transfers between devices with their start and end apart: 24 -> 0, of which waited for: 20 -> 0; matrix products, arithmetic and copies ran while one was open for 6% -> 0% of each run, Pallas kernels for 0% -> 0%
where the time goes in v1:
time: 61.4 us; the launch traced here: 61.2 us
  Pallas kernels  53.3 us (87%)
  local copies, waits for them, and re-layouts  7.19 us (12%)
  between operations  0.66 us (1%)
    pallas_call x1, Pallas kernels, on_device(): pl.pallas_call(functools.partial(kernel, n_lat, n_lon), out_shape=(jax.Sh...  53.3 us
    unnamed x13, local copies, waits for them, and re-layouts  4.78 us
    pallas_call x2, local copies, waits for them, and re-layouts, on_device(): pl.pallas_call(functools.partial(kernel, n_lat, n_lon), out_shape=(jax.Sh...  2.41 us

profile of v1, /device:TPU:6, one launch (start us, length us, event | category | flops | bytes accessed | tf_op | source)
XLA Modules:
  0.0 61.2 jit_solution(15943927222350037524)
XLA Ops:
  0.6 0.0 copy-start.3
  0.6 1.3 %copy.14.ce_hbm = s32[1,3,640]{2,1,0:T(4,128)} copy(s32[1,3,640]{2,0,1:T(1,128)} %param.13) | data formatting | bytes 15360 | tf_op args[3]
  1.9 0.0 copy-done.3
  1.9 0.0 copy-start.2
  1.9 0.6 copy.15.w_hbm
  2.5 0.0 copy-start.1
  2.5 1.6 %copy.12.p_hbm = f32[1,30,640]{2,1,0:T(8,128)} copy(f32[1,30,640]{2,0,1:T(1,128)} %param.10) | data formatting | bytes 153600 | tf_op args[0]
  4.1 0.0 copy-done.2
  4.1 0.6 %copy.16.cp_hbm = f32[1,30,640]{2,1,0:T(8,128)} copy(f32[1,30,640]{2,0,1:T(1,128)S(1)} %copy-done.2) | data formatting | bytes 153600 | tf_op args[9]
  4.7 0.0 copy-done.1
  4.7 0.7 %copy.13.v_hbm = f32[1,30,960]{2,1,0:T(8,128)} copy(f32[1,30,960]{2,0,1:T(1,128)S(1)} %copy-done.1) | data formatting | bytes 230400 | tf_op args[1]
  5.4 53.3 %shard_map.113 = (f32[1,30,640]{2,1,0:T(8,128)}, f32[1,30,960]{2,1,0:T(8,128)}) custom-call(f32[1,30,640]{2,1,0:T(8,128)} %copy.12.p_hbm, f32[1,30,960]{2,1,0:T(8,128)} %copy.13.v_hbm, s32[1,2,960]{2,1,0:T(2,128)} %ec_hbm.1, s32[1,3,640]{2,1,0:T(4,128)} %copy.14.ce_hbm, s32[1,8,128]{2,1,0:T(8,128)} %sc_hbm.1, s32[1,8,128]{2,1,0:T(8,128)} %se_hbm.1, ...), custom_call_target="tpu_custom_call" | custom-call | tf_op jit(solution)/shard_map/pallas_call | solution.py:325
  58.8 0.0 copy-start
  58.8 1.6 %copy.17 = f32[1,30,640]{2,0,1:T(1,128)} copy(f32[1,30,640]{2,1,0:T(8,128)} %get-tuple-element.2) | data formatting | bytes 153600 | tf_op jit(solution)/shard_map/pallas_call | solution.py:325
  60.4 0.0 copy-done
  60.4 0.8 %copy.18 = f32[1,30,960]{2,0,1:T(1,128)} copy(f32[1,30,960]{2,1,0:T(8,128)S(1)} %copy-done) | data formatting | bytes 230400 | tf_op jit(solution)/shard_map/pallas_call | solution.py:325
Async XLA Ops:
  0.6 1.3 %copy-start.3 = (f32[1,3,640]{2,0,1:T(1,128)S(1)}, f32[1,3,640]{2,0,1:T(1,128)}, u32[]{:S(2)}) copy-start(f32[1,3,640]{2,0,1:T(1,128)} %param.17) | copy-start | bytes 23044
  1.9 2.2 %copy-start.2 = (f32[1,30,640]{2,0,1:T(1,128)S(1)}, f32[1,30,640]{2,0,1:T(1,128)}, u32[]{:S(2)}) copy-start(f32[1,30,640]{2,0,1:T(1,128)} %param.19) | copy-start | bytes 230404
  2.5 2.2 %copy-start.1 = (f32[1,30,960]{2,0,1:T(1,128)S(1)}, f32[1,30,960]{2,0,1:T(1,128)}, u32[]{:S(2)}) copy-start(f32[1,30,960]{2,0,1:T(1,128)} %param.11) | copy-start | bytes 345604
  58.8 1.6 %copy-start = (f32[1,30,960]{2,1,0:T(8,128)S(1)}, f32[1,30,960]{2,1,0:T(8,128)}, u32[]{:S(2)}) copy-start(f32[1,30,960]{2,1,0:T(8,128)} %get-tuple-element.3) | copy-start | bytes 345604

commit v2 on v1

--- a/solution.py
+++ b/solution.py
@@ -16,7 +16,6 @@
 LP = 32
 N = 8 * H
 DIRECTIONS = ((-1, -1), (-1, 0), (-1, 1), (0, -1), (0, 1), (1, -1), (1, 0), (1, 1))
-ORDER = (0, 2, 5, 7, 1, 6, 3, 4)
 F32, BF16 = jnp.float32, jnp.bfloat16
 MESH = pl.DeviceIdType.MESH
 
@@ -42,14 +41,24 @@
     pres, vel, pieces_out, pieces_in,
     pres_hl, vel_hl, pick_c, pick_e, diff, diff_l, weight,
     rows_l, grad_l, vel_l, right, solve_in, solve_mid, coef_a, coef_b, coef_r,
-    in_sem, out_sem, send_sem, recv_sem,
+    in_sem, send_sem, recv_sem,
 ):
     a, b = lax.axis_index("lat"), lax.axis_index("lon")
     not_first, not_last = a > 0, a < n_lat - 1
 
+    def device_at(p, q):
+        return (a + p, lax.rem(b + q + n_lon, n_lon))
+
     def neighbour(member):
-        p, q = DIRECTIONS[member]
-        return (a + p, lax.rem(b + q + n_lon, n_lon))
+        return device_at(*DIRECTIONS[member])
+
+    core = lax.rem(b, 2)
+    cross = 2 * core - 1
+    order = (
+        (-1, cross, 2 * core), (1, cross, 5 + 2 * core),
+        (-1, -cross, 2 - 2 * core), (1, -cross, 7 - 2 * core),
+        (-1, 0, 1), (1, 0, 6), (0, cross, 3 + core), (0, -cross, 4 - core),
+    )
 
     barrier = pltpu.get_barrier_semaphore()
 
@@ -65,27 +74,34 @@
     targets = (sc_in, p_in, se_in, v_in, ec_in, inv_in, ce_in, w_in, ss_in, cp_in)
     loads = []
     for i, (source, target) in enumerate(zip(sources, targets)):
-        view = source if source.ndim == 2 else source.at[0]
+        if source.ndim == 2:
+            view = source
+        else:
+            view = source.at[0] if source.shape[0] == 1 else source.at[:, 0, :]
         loads.append(pltpu.make_async_copy(view, target, in_sem.at[i]))
         loads[-1].start()
 
-    def copy(exchange, member):
+    def copy(exchange, turn):
+        p, q, member = order[turn]
         return pltpu.make_async_remote_copy(
-            src_ref=pieces_out.at[exchange, member],
+            src_ref=pieces_out.at[exchange, turn],
             dst_ref=pieces_in.at[exchange, 7 - member],
-            send_sem=send_sem.at[exchange, member],
+            send_sem=send_sem.at[exchange, turn],
             recv_sem=recv_sem.at[exchange, 7 - member],
-            device_id=neighbour(member),
+            device_id=device_at(p, q),
             device_id_type=MESH,
         )
 
-    def by_row(members, action):
-        for member in members:
-            row = DIRECTIONS[member][0]
+    def each(turns, action):
+        for turn in turns:
+            row = order[turn][0]
             if row == 0:
-                action(member)
+                action(turn)
             else:
-                pl.when(not_first if row < 0 else not_last)(functools.partial(action, member))
+                pl.when(not_first if row < 0 else not_last)(functools.partial(action, turn))
+
+    def send(exchange, turns):
+        each(turns, lambda turn: copy(exchange, turn).start())
 
     def receive(exchange, members, target, base):
         for member in members:
@@ -99,55 +115,85 @@
             ).wait_recv()
         for member in members:
             high, low = split(pieces_in[exchange, member])
-            target[:LP, base + member * H:base + (member + 1) * H] = high
-            target[LP:, base + member * H:base + (member + 1) * H] = low
+            target[:L, base + member * H:base + (member + 1) * H] = high
+            target[LP:LP + L, base + member * H:base + (member + 1) * H] = low
 
     def receive_rest(exchange, target, base):
         pl.when(not_first)(lambda: receive(exchange, (0, 1, 2), target, base))
         pl.when(not_last)(lambda: receive(exchange, (5, 6, 7), target, base))
 
-    def one_hot_rows(start, count, width):
-        return (lax.broadcasted_iota(jnp.int32, (count, width), 0) + start).astype(F32)
+    def in_blocks(count, build):
+        def step(block, carry):
+            start = pl.multiple_of(block * H, H)
+            base = start.astype(F32)
+
+            def local(places):
+                within = places - base
+                within = jnp.where((within >= 0.0) & (within < float(H)), within, -1.0)
+                return jnp.broadcast_to(within, (16, places.shape[1])).astype(BF16)
+
+            build(start, local)
+            return carry
+
+        lax.fori_loop(0, count // H, step, 0)
+
+    def row_numbers(j, width):
+        return (lax.broadcasted_iota(jnp.int32, (16, width), 0) + 16 * j).astype(F32).astype(BF16)
 
     def build_pick(lists_ref, target, own):
         lists = lists_ref[...].astype(F32)
-        picks = jnp.concatenate([lists[member:member + 1] for member in ORDER], axis=1)
-
-        def step(i, carry):
-            start = pl.multiple_of(i * 32, 32)
-            hit = one_hot_rows(start, 32, N) == picks
-            target[pl.ds(start, 32), :] = jnp.where(hit, 1.0, 0.0).astype(BF16)
-            return carry
-
-        lax.fori_loop(0, own // 32, step, 0)
+
+        def either(first, second):
+            return jnp.where(core == 0, lists[first:first + 1], lists[second:second + 1])
+
+        picks = jnp.concatenate(
+            [either(0, 2), either(5, 7), either(2, 0), either(7, 5),
+             lists[1:2], lists[6:7], either(3, 4), either(4, 3)], axis=1)
+
+        def build(start, local):
+            here = local(picks)
+            one, zero = jnp.ones((16, N), BF16), jnp.zeros((16, N), BF16)
+            for j in range(H // 16):
+                target[pl.ds(start + 16 * j, 16), :] = jnp.where(row_numbers(j, N) == here, one, zero)
+
+        in_blocks(own, build)
 
     def build_diff(first, second, target):
-        def step(i, carry):
-            start = pl.multiple_of(i * 32, 32)
-            rows = one_hot_rows(start, 32, N)
-            hit = jnp.where(rows == second, 1.0, 0.0) - jnp.where(rows == first, 1.0, 0.0)
-            target[pl.ds(start, 32), :] = hit.astype(BF16)
-            return carry
-
-        lax.fori_loop(0, (C + N) // 32, step, 0)
+        def build(start, local):
+            minus, plus = local(first), local(second)
+            one, zero = jnp.ones((16, N), BF16), jnp.zeros((16, N), BF16)
+            for j in range(H // 16):
+                rows = row_numbers(j, N)
+                hit = jnp.where(rows == plus, one, zero) - jnp.where(rows == minus, one, zero)
+                target[pl.ds(start + 16 * j, 16), :] = hit
+
+        in_blocks(C + N, build)
 
     def build_weight():
         places = ce_in[...].astype(F32)
         places = jnp.where(places >= E, places + (EP - E), places)
         weights = w_in[...] * ss_in[...]
-
-        def step(i, carry):
-            start = pl.multiple_of(i * 32, 32)
-            rows = one_hot_rows(start, 32, C)
-            total = jnp.where(rows == places[0:1], weights[0:1], 0.0)
-            total = total + jnp.where(rows == places[1:2], weights[1:2], 0.0)
-            total = total + jnp.where(rows == places[2:3], weights[2:3], 0.0)
-            high, low = split(total)
-            weight[pl.ds(start, 32), :C] = high
-            weight[pl.ds(start, 32), C:] = low
-            return carry
-
-        lax.fori_loop(0, (EP + N) // 32, step, 0)
+        place = [places[j:j + 1] for j in range(3)]
+        factor = [weights[j:j + 1] for j in range(3)]
+        for i, j in ((0, 1), (0, 2), (1, 2)):
+            same = place[i] == place[j]
+            factor[i] = factor[i] + jnp.where(same, factor[j], 0.0)
+            place[j] = jnp.where(same, -1.0, place[j])
+        parts = [split(jnp.broadcast_to(x, (16, C))) for x in factor]
+
+        def build(start, local):
+            here = [local(x) for x in place]
+            zero = jnp.zeros((16, C), BF16)
+            for j in range(H // 16):
+                rows = row_numbers(j, C)
+                high, low = zero, zero
+                for where, (part_high, part_low) in zip(here, parts):
+                    hit = rows == where
+                    high, low = jnp.where(hit, part_high, high), jnp.where(hit, part_low, low)
+                weight[pl.ds(start + 16 * j, 16), :C] = high
+                weight[pl.ds(start + 16 * j, 16), C:] = low
+
+        in_blocks(EP + N, build)
 
     def to_columns(x, target):
         for block in range(C // H):
@@ -187,12 +233,16 @@
             pres_hl[:LP, block * H:(block + 1) * H] = high
             pres_hl[LP:, block * H:(block + 1) * H] = low
 
-    def pressure_pieces(exchange):
+    def put_pieces(exchange, chunk, x):
+        for half in range(2):
+            pieces_out[exchange, 2 * chunk + half] = x[:L, half * H:(half + 1) * H]
+
+    def pressure_pieces(exchange, at_once):
         for chunk in range(4):
             cols = slice(chunk * 256, chunk * 256 + 256)
-            picked = halves(dot(pres_hl[:, :C], pick_c[:, cols]))
-            for half in range(2):
-                pieces_out[exchange, ORDER[2 * chunk + half]] = picked[:, half * H:(half + 1) * H]
+            put_pieces(exchange, chunk, halves(dot(pres_hl[:, :C], pick_c[:, cols])))
+            if at_once:
+                send(exchange, (2 * chunk, 2 * chunk + 1))
 
     def own_gradient():
         for chunk in range(4):
@@ -208,9 +258,9 @@
     pres_hl[:LP, :C] = high
     pres_hl[LP:, :C] = low
     pres_hl[:, C:] = jnp.zeros((2 * LP, N), BF16)
-    pressure_pieces(0)
+    pressure_pieces(0, False)
     pl.semaphore_wait(barrier, 2 + 3 * lax.min(a, 1) + 3 * lax.min(n_lat - 1 - a, 1))
-    by_row(ORDER, lambda member: copy(0, member).start())
+    send(0, range(8))
 
     loads[2].wait()
     build_pick(se_in, pick_e, EP)
@@ -262,9 +312,8 @@
             far = far + dot(pres_hl[:, ahead], diff_l[ahead, cols])
             moved = vel_l[:, cols] - rows_l[6:7, cols] * (grad_l[:, cols] + halves(far))
             vel_l[:, cols] = moved
-            for half in range(2):
-                pieces_out[second, ORDER[2 * chunk + half]] = moved[:, half * H:(half + 1) * H]
-            by_row(ORDER[2 * chunk:2 * chunk + 2], lambda member: copy(second, member).start())
+            put_pieces(second, chunk, moved)
+            send(second, (2 * chunk, 2 * chunk + 1))
 
         for chunk in range(4):
             cols = slice(chunk * 256, chunk * 256 + 256)
@@ -282,8 +331,7 @@
 
         @pl.when(s == NSUB - 1)
         def _():
-            v_in[...] = vel[:L, :E]
-            pltpu.make_async_copy(v_in, v_out.at[0], out_sem.at[0]).start()
+            v_out[...] = vel[:L, :E]
 
         def divergence(places):
             wide = dot(vel_hl[:, places], weight[places, :])
@@ -299,20 +347,26 @@
 
         @pl.when(s < NSUB - 1)
         def _():
-            pressure_pieces(second + 1)
-            by_row(ORDER, lambda member: copy(second + 1, member).start())
+            pressure_pieces(second + 1, True)
             own_gradient()
 
         return carry
 
     lax.fori_loop(0, NSUB, substep, 0)
-    p_in[...] = pres[:L, :]
-    pressure_store = pltpu.make_async_copy(p_in, p_out.at[0], out_sem.at[1])
-    pressure_store.start()
+    p_out[...] = pres[:L, :]
     for exchange in range(2 * NSUB):
-        by_row(ORDER, lambda member: copy(exchange, member).wait_send())
-    pltpu.make_async_copy(v_in, v_out.at[0], out_sem.at[0]).wait()
-    pressure_store.wait()
+        each(range(8), lambda turn: copy(exchange, turn).wait_send())
+
+
+def store(p, v, p_out, v_out, sem):
+    copies = [
+        pltpu.make_async_copy(p, p_out.at[:, 0, :], sem.at[0]),
+        pltpu.make_async_copy(v, v_out.at[:, 0, :], sem.at[1]),
+    ]
+    for copy in copies:
+        copy.start()
+    for copy in copies:
+        copy.wait()
 
 
 def solution(mesh):
@@ -321,34 +375,49 @@
     vmem = pltpu.VMEM
     i32 = jnp.int32
 
-    def on_device(*operands):
-        return pl.pallas_call(
+    def turned(x):
+        return jnp.transpose(x, (1, 0, 2))
+
+    def on_device(p, v, ec, ce, sc, se, inv, w, ss, cp):
+        results = pl.pallas_call(
             functools.partial(kernel, n_lat, n_lon),
             out_shape=(
-                jax.ShapeDtypeStruct((1, L, C), F32),
-                jax.ShapeDtypeStruct((1, L, E), F32),
+                vmem((L, C), F32),
+                vmem((L, E), F32),
             ),
             in_specs=[any_space] * 10,
-            out_specs=(any_space, any_space),
+            out_specs=(pl.BlockSpec(memory_space=vmem),) * 2,
             scratch_shapes=[
                 vmem((L, C), F32), vmem((L, E), F32),
                 vmem((2, E), i32), vmem((3, C), i32), vmem((8, H), i32), vmem((8, H), i32),
                 vmem((1, E), F32), vmem((3, C), F32), vmem((1, C), F32), vmem((L, C), F32),
                 vmem((LP, C), F32), vmem((LP, EP), F32),
-                vmem((2 * NSUB, 8, LP, H), F32), vmem((2 * NSUB, 8, LP, H), F32),
+                vmem((2 * NSUB, 8, L, H), F32), vmem((2 * NSUB, 8, L, H), F32),
                 vmem((2 * LP, C + N), BF16), vmem((2 * LP, EP + N), BF16),
                 vmem((C, N), BF16), vmem((EP, N), BF16),
                 vmem((C + N, N), BF16), vmem((C + N, N), BF16), vmem((EP + N, 2 * C), BF16),
                 vmem((8, N), F32), vmem((LP, N), F32), vmem((LP, N), F32), vmem((LP, C), F32),
                 vmem((8 * LP, H), F32), vmem((8 * LP, H), F32),
                 vmem((8 * LP, H), F32), vmem((8 * LP, H), F32), vmem((8 * LP, H), F32),
-                pltpu.SemaphoreType.DMA((10,)), pltpu.SemaphoreType.DMA((2,)),
+                pltpu.SemaphoreType.DMA((10,)),
                 pltpu.SemaphoreType.DMA((2 * NSUB, 8)), pltpu.SemaphoreType.DMA((2 * NSUB, 8)),
             ],
             compiler_params=pltpu.CompilerParams(
                 collective_id=0, has_side_effects=True, vmem_limit_bytes=60 * 1024 * 1024
             ),
-        )(*operands)
+        )(turned(p), turned(v), ec, turned(ce), sc, se, inv, turned(w), ss, turned(cp))
+        stored = pl.pallas_call(
+            store,
+            out_shape=(
+                jax.ShapeDtypeStruct((L, 1, C), F32),
+                jax.ShapeDtypeStruct((L, 1, E), F32),
+            ),
+            in_specs=[pl.BlockSpec(memory_space=vmem)] * 2,
+            out_specs=(any_space, any_space),
+            scratch_shapes=[pltpu.SemaphoreType.DMA((2,))],
+            compiler_params=pltpu.CompilerParams(vmem_limit_bytes=1024 * 1024),
+        )(*results)
+        return tuple(turned(x) for x in stored)
 
     spec3, spec2 = P("lat", None, "lon"), P("lat", "lon")
     return jax.shard_map(

time: 61.4 us -> 52.2 us (0.85)
  local copies, waits for them, and re-layouts: 7.19 us -> 0 us
  Pallas kernels: 53.3 us -> 51.4 us
    unnamed x13 -> x0, local copies, waits for them, and re-layouts: 4.78 us -> none
    pallas_call x2 -> x0, local copies, waits for them, and re-layouts: 2.41 us -> none  [on_device(): pl.pallas_call(functools.partial(kernel, n_lat, n_lon), out_shape=(jax.Sh...]
    pallas_call x1 -> x2, Pallas kernels: 53.3 us -> 51.4 us  [the longest x1 50.7 us: on_device(): pl.pallas_call(functools.partial(kernel, n_lat, n_lon), out_shape=(vmem((...]
where the time goes in v2:
time: 52.2 us; the launch traced here: 52 us
  Pallas kernels  51.4 us (98%)
  between operations  0.64 us (1%)
    pallas_call x1, Pallas kernels, on_device(): pl.pallas_call(functools.partial(kernel, n_lat, n_lon), out_shape=(vmem((...  50.7 us

profile of v2, /device:TPU:6, one launch (start us, length us, event | category | flops | bytes accessed | tf_op | source)
XLA Modules:
  0.0 52.0 jit_solution(11082255575485271721)
XLA Ops:
  0.6 50.7 %shard_map.113 = (f32[30,640]{1,0:T(8,128)S(1)}, f32[30,960]{1,0:T(8,128)S(1)}) custom-call(f32[30,1,640]{2,1,0:T(1,128)} %bitcast.8, f32[30,1,960]{2,1,0:T(1,128)} %bitcast.7, s32[1,2,960]{2,1,0:T(2,128)} %ec_hbm.1, s32[3,1,640]{2,1,0:T(1,128)} %bitcast.10, s32[1,8,128]{2,1,0:T(8,128)} %sc_hbm.1, s32[1,8,128]{2,1,0:T(8,128)} %se_hbm.1, f32[1,960]{1,0:T(1,128)} %inv_hbm.1, ...), custom_call_target="tpu_custom_call" | custom-call | tf_op jit(solution)/shard_map/pallas_call | solution.py:382
  51.3 0.7 %shard_map.114 = (f32[30,1,640]{2,1,0:T(1,128)}, f32[30,1,960]{2,1,0:T(1,128)}) custom-call(f32[30,640]{1,0:T(8,128)S(1)} %get-tuple-element.6.p, f32[30,960]{1,0:T(8,128)S(1)} %get-tuple-element.7.v), custom_call_target="tpu_custom_call" | custom-call | tf_op jit(solution)/shard_map/pallas_call | solution.py:409

commit v3 on v2

--- a/solution.py
+++ b/solution.py
@@ -13,6 +13,7 @@
 EP = 1024
 H = 128
 L = 30
+MID = L // 2
 LP = 32
 N = 8 * H
 DIRECTIONS = ((-1, -1), (-1, 0), (-1, 1), (0, -1), (0, 1), (1, -1), (1, 0), (1, 1))
@@ -60,16 +61,6 @@
         (-1, 0, 1), (1, 0, 6), (0, cross, 3 + core), (0, -cross, 4 - core),
     )
 
-    barrier = pltpu.get_barrier_semaphore()
-
-    def greet(members):
-        for member in members:
-            pl.semaphore_signal(barrier, inc=1, device_id=neighbour(member), device_id_type=MESH)
-
-    greet((3, 4))
-    pl.when(not_first)(lambda: greet((0, 1, 2)))
-    pl.when(not_last)(lambda: greet((5, 6, 7)))
-
     sources = (sc_hbm, p_hbm, se_hbm, v_hbm, ec_hbm, inv_hbm, ce_hbm, w_hbm, ss_hbm, cp_hbm)
     targets = (sc_in, p_in, se_in, v_in, ec_in, inv_in, ce_in, w_in, ss_in, cp_in)
     loads = []
@@ -79,7 +70,21 @@
         else:
             view = source.at[0] if source.shape[0] == 1 else source.at[:, 0, :]
         loads.append(pltpu.make_async_copy(view, target, in_sem.at[i]))
-        loads[-1].start()
+    loads[0].start()
+    loads[1].start()
+
+    barrier = pltpu.get_barrier_semaphore()
+
+    def greet(members):
+        for member in members:
+            pl.semaphore_signal(barrier, inc=1, device_id=neighbour(member), device_id_type=MESH)
+
+    greet((3, 4))
+    pl.when(not_first)(lambda: greet((0, 1, 2)))
+    pl.when(not_last)(lambda: greet((5, 6, 7)))
+
+    for load in loads[2:]:
+        load.start()
 
     def copy(exchange, turn):
         p, q, member = order[turn]
@@ -103,24 +108,34 @@
     def send(exchange, turns):
         each(turns, lambda turn: copy(exchange, turn).start())
 
-    def receive(exchange, members, target, base):
-        for member in members:
+    def receive(exchange, first, count, target, base):
+        for i in range(count):
             pltpu.make_async_remote_copy(
-                src_ref=pieces_out.at[exchange, member],
-                dst_ref=pieces_in.at[exchange, member],
-                send_sem=send_sem.at[exchange, member],
-                recv_sem=recv_sem.at[exchange, member],
-                device_id=neighbour(member),
+                src_ref=pieces_out.at[exchange, i],
+                dst_ref=pieces_in.at[exchange, first + i],
+                send_sem=send_sem.at[exchange, i],
+                recv_sem=recv_sem.at[exchange, first + i],
+                device_id=device_at(0, 1),
                 device_id_type=MESH,
             ).wait_recv()
-        for member in members:
-            high, low = split(pieces_in[exchange, member])
-            target[:L, base + member * H:base + (member + 1) * H] = high
-            target[LP:LP + L, base + member * H:base + (member + 1) * H] = low
-
-    def receive_rest(exchange, target, base):
-        pl.when(not_first)(lambda: receive(exchange, (0, 1, 2), target, base))
-        pl.when(not_last)(lambda: receive(exchange, (5, 6, 7), target, base))
+        for i in range(count):
+            high, low = split(pieces_in[exchange, first + i])
+            cols = pl.ds(pl.multiple_of(base + (first + i) * H, H), H)
+            target[:L, cols] = high
+            target[LP:LP + L, cols] = low
+
+    ahead_first = 1 - lax.min(lax.rem(a, 4), 1)
+    groups = (
+        (5 * ahead_first, jnp.where(ahead_first == 1, not_last, not_first)),
+        (5 - 5 * ahead_first, jnp.where(ahead_first == 1, not_first, not_last)),
+    )
+
+    def receive_group(exchange, group, target, base):
+        first, there = groups[group]
+        pl.when(there)(lambda: receive(exchange, first, 3, target, base))
+
+    def group_places(group, base):
+        return pl.ds(pl.multiple_of(base + groups[group][0] * H, H), 3 * H)
 
     def in_blocks(count, build):
         def step(block, carry):
@@ -202,30 +217,63 @@
     def build_solver():
         coupling = jnp.concatenate([cp_in[...], jnp.zeros((LP - L, C), F32)], axis=0)
         to_columns(coupling, solve_in)
-        below, inverse = None, None
-        for k in range(L):
-            here = solve_in[8 * k:8 * k + 8, :]
-            divisor = 1.0 + here
+
+        def rows(k):
+            return slice(8 * k, 8 * k + 8)
+
+        inverse = None
+        for k in range(MID):
+            above = solve_in[rows(k), :]
+            divisor = 1.0 + above
             if k > 0:
+                below = solve_in[rows(k - 1), :]
                 divisor = divisor + below - below * (below * inverse)
             inverse = 1.0 / divisor
-            coef_a[8 * k:8 * k + 8, :] = inverse
+            coef_a[rows(k), :] = inverse
             if k > 0:
-                coef_b[8 * k:8 * k + 8, :] = below * inverse
-            coef_r[8 * k:8 * k + 8, :] = here * inverse
-            below = here
+                coef_b[rows(k), :] = below * inverse
+            coef_r[rows(k), :] = above * inverse
+        inverse = None
+        for k in range(L - 1, MID - 1, -1):
+            above, below = solve_in[rows(k), :], solve_in[rows(k - 1), :]
+            divisor = 1.0 + above + below
+            if k < L - 1:
+                divisor = divisor - above * (above * inverse)
+            inverse = 1.0 / divisor
+            coef_a[rows(k), :] = inverse
+            if k < L - 1:
+                coef_b[rows(k), :] = above * inverse
+            coef_r[rows(k), :] = below * inverse
+        coef_b[rows(0), :] = 1.0 / (1.0 - coef_r[rows(MID - 1), :] * coef_r[rows(MID), :])
 
     def solve():
-        current = solve_in[0:8, :] * coef_a[0:8, :]
-        solve_mid[0:8, :] = current
-        for k in range(1, L):
-            rows = slice(8 * k, 8 * k + 8)
-            current = solve_in[rows, :] * coef_a[rows, :] + coef_b[rows, :] * current
-            solve_mid[rows, :] = current
-        for k in range(L - 2, -1, -1):
-            rows = slice(8 * k, 8 * k + 8)
-            current = solve_mid[rows, :] + coef_r[rows, :] * current
-            solve_mid[rows, :] = current
+        def rows(k):
+            return slice(8 * k, 8 * k + 8)
+
+        low = solve_in[rows(0), :] * coef_a[rows(0), :]
+        high = solve_in[rows(L - 1), :] * coef_a[rows(L - 1), :]
+        solve_mid[rows(0), :] = low
+        solve_mid[rows(L - 1), :] = high
+        for k in range(1, MID):
+            up, down = rows(k), rows(L - 1 - k)
+            low = solve_in[up, :] * coef_a[up, :] + coef_b[up, :] * low
+            high = solve_in[down, :] * coef_a[down, :] + coef_b[down, :] * high
+            if k < MID - 1:
+                solve_mid[up, :] = low
+                solve_mid[down, :] = high
+        meet = coef_b[rows(0), :]
+        low, high = (
+            (low + coef_r[rows(MID - 1), :] * high) * meet,
+            (high + coef_r[rows(MID), :] * low) * meet,
+        )
+        solve_mid[rows(MID - 1), :] = low
+        solve_mid[rows(MID), :] = high
+        for k in range(MID - 2, -1, -1):
+            up, down = rows(k), rows(L - 1 - k)
+            low = solve_mid[up, :] + coef_r[up, :] * low
+            high = solve_mid[down, :] + coef_r[down, :] * high
+            solve_mid[up, :] = low
+            solve_mid[down, :] = high
         for block in range(C // H):
             x = solve_mid[pl.ds(block, LP, stride=8), :]
             pres[:, block * H:(block + 1) * H] = x
@@ -237,12 +285,11 @@
         for half in range(2):
             pieces_out[exchange, 2 * chunk + half] = x[:L, half * H:(half + 1) * H]
 
-    def pressure_pieces(exchange, at_once):
+    def pressure_pieces(exchange):
         for chunk in range(4):
             cols = slice(chunk * 256, chunk * 256 + 256)
             put_pieces(exchange, chunk, halves(dot(pres_hl[:, :C], pick_c[:, cols])))
-            if at_once:
-                send(exchange, (2 * chunk, 2 * chunk + 1))
+            send(exchange, (2 * chunk, 2 * chunk + 1))
 
     def own_gradient():
         for chunk in range(4):
@@ -258,9 +305,8 @@
     pres_hl[:LP, :C] = high
     pres_hl[LP:, :C] = low
     pres_hl[:, C:] = jnp.zeros((2 * LP, N), BF16)
-    pressure_pieces(0, False)
     pl.semaphore_wait(barrier, 2 + 3 * lax.min(a, 1) + 3 * lax.min(n_lat - 1 - a, 1))
-    send(0, range(8))
+    pressure_pieces(0)
 
     loads[2].wait()
     build_pick(se_in, pick_e, EP)
@@ -299,18 +345,21 @@
 
     def substep(s, carry):
         first, second = 2 * s, 2 * s + 1
-        receive(first, (3, 4), pres_hl, C)
-        near = slice(C + 3 * H, C + 5 * H)
+        def add_gradient(places):
+            for chunk in range(4):
+                cols = slice(chunk * 256, chunk * 256 + 256)
+                grad_l[:, cols] = grad_l[:, cols] + halves(dot(pres_hl[:, places], diff_l[places, cols]))
+
+        receive(first, 3, 2, pres_hl, C)
+        add_gradient(slice(C + 3 * H, C + 5 * H))
+        receive_group(first, 0, pres_hl, C)
+        add_gradient(group_places(0, C))
+        receive_group(first, 1, pres_hl, C)
+        places = group_places(1, C)
         for chunk in range(4):
             cols = slice(chunk * 256, chunk * 256 + 256)
-            grad_l[:, cols] = grad_l[:, cols] + halves(dot(pres_hl[:, near], diff_l[near, cols]))
-        receive_rest(first, pres_hl, C)
-        behind, ahead = slice(C, C + 3 * H), slice(C + 5 * H, C + 8 * H)
-        for chunk in range(4):
-            cols = slice(chunk * 256, chunk * 256 + 256)
-            far = dot(pres_hl[:, behind], diff_l[behind, cols])
-            far = far + dot(pres_hl[:, ahead], diff_l[ahead, cols])
-            moved = vel_l[:, cols] - rows_l[6:7, cols] * (grad_l[:, cols] + halves(far))
+            gradient = grad_l[:, cols] + halves(dot(pres_hl[:, places], diff_l[places, cols]))
+            moved = vel_l[:, cols] - rows_l[6:7, cols] * gradient
             vel_l[:, cols] = moved
             put_pieces(second, chunk, moved)
             send(second, (2 * chunk, 2 * chunk + 1))
@@ -338,16 +387,17 @@
             return halves(wide[:, :C] + wide[:, C:])
 
         right[...] = pres[...] - divergence(slice(0, EP))
-        receive(second, (3, 4), vel_hl, EP)
+        receive(second, 3, 2, vel_hl, EP)
         right[...] = right[...] - divergence(slice(EP + 3 * H, EP + 5 * H))
-        receive_rest(second, vel_hl, EP)
-        total = divergence(slice(EP, EP + 3 * H)) + divergence(slice(EP + 5 * H, EP + 8 * H))
-        to_columns(right[...] - total, solve_in)
+        receive_group(second, 0, vel_hl, EP)
+        right[...] = right[...] - divergence(group_places(0, EP))
+        receive_group(second, 1, vel_hl, EP)
+        to_columns(right[...] - divergence(group_places(1, EP)), solve_in)
         solve()
 
         @pl.when(s < NSUB - 1)
         def _():
-            pressure_pieces(second + 1, True)
+            pressure_pieces(second + 1)
             own_gradient()
 
         return carry

time: 52.2 us -> 51.7 us (level)
    pallas_call x1, Pallas kernels: 50.7 us -> 50.2 us  [on_device(): pl.pallas_call(functools.partial(kernel, n_lat, n_lon), out_shape=(vmem((...]
where the time goes in v3:
time: 51.7 us; the launch traced here: 51.5 us
  Pallas kernels  50.9 us (98%)
  between operations  0.64 us (1%)
    pallas_call x1, Pallas kernels, on_device(): pl.pallas_call(functools.partial(kernel, n_lat, n_lon), out_shape=(vmem((...  50.2 us

profile of v3, /device:TPU:6, one launch (start us, length us, event | category | flops | bytes accessed | tf_op | source)
XLA Modules:
  0.0 51.5 jit_solution(4201926813207175451)
XLA Ops:
  0.6 50.2 %shard_map.113 = (f32[30,640]{1,0:T(8,128)S(1)}, f32[30,960]{1,0:T(8,128)S(1)}) custom-call(f32[30,1,640]{2,1,0:T(1,128)} %bitcast.8, f32[30,1,960]{2,1,0:T(1,128)} %bitcast.7, s32[1,2,960]{2,1,0:T(2,128)} %ec_hbm.1, s32[3,1,640]{2,1,0:T(1,128)} %bitcast.10, s32[1,8,128]{2,1,0:T(8,128)} %sc_hbm.1, s32[1,8,128]{2,1,0:T(8,128)} %se_hbm.1, f32[1,960]{1,0:T(1,128)} %inv_hbm.1, ...), custom_call_target="tpu_custom_call" | custom-call | tf_op jit(solution)/shard_map/pallas_call | solution.py:432
  50.8 0.7 %shard_map.114 = (f32[30,1,640]{2,1,0:T(1,128)}, f32[30,1,960]{2,1,0:T(1,128)}) custom-call(f32[30,640]{1,0:T(8,128)S(1)} %get-tuple-element.6.p, f32[30,960]{1,0:T(8,128)S(1)} %get-tuple-element.7.v), custom_call_target="tpu_custom_call" | custom-call | tf_op jit(solution)/shard_map/pallas_call | solution.py:459

commit v4 on v3

--- a/solution.py
+++ b/solution.py
@@ -281,15 +281,15 @@
             pres_hl[:LP, block * H:(block + 1) * H] = high
             pres_hl[LP:, block * H:(block + 1) * H] = low
 
-    def put_pieces(exchange, chunk, x):
-        for half in range(2):
-            pieces_out[exchange, 2 * chunk + half] = x[:L, half * H:(half + 1) * H]
+    def put_and_send(exchange, chunks):
+        for chunk, x in enumerate(chunks):
+            for half in range(2):
+                pieces_out[exchange, 2 * chunk + half] = x[:L, half * H:(half + 1) * H]
+            send(exchange, (2 * chunk, 2 * chunk + 1))
 
     def pressure_pieces(exchange):
-        for chunk in range(4):
-            cols = slice(chunk * 256, chunk * 256 + 256)
-            put_pieces(exchange, chunk, halves(dot(pres_hl[:, :C], pick_c[:, cols])))
-            send(exchange, (2 * chunk, 2 * chunk + 1))
+        products = [dot(pres_hl[:, :C], pick_c[:, chunk * 256:chunk * 256 + 256]) for chunk in range(4)]
+        put_and_send(exchange, [halves(x) for x in products])
 
     def own_gradient():
         for chunk in range(4):
@@ -345,24 +345,24 @@
 
     def substep(s, carry):
         first, second = 2 * s, 2 * s + 1
-        def add_gradient(places):
-            for chunk in range(4):
-                cols = slice(chunk * 256, chunk * 256 + 256)
-                grad_l[:, cols] = grad_l[:, cols] + halves(dot(pres_hl[:, places], diff_l[places, cols]))
-
         receive(first, 3, 2, pres_hl, C)
-        add_gradient(slice(C + 3 * H, C + 5 * H))
         receive_group(first, 0, pres_hl, C)
-        add_gradient(group_places(0, C))
+        near, places = slice(C + 3 * H, C + 5 * H), group_places(0, C)
+        for chunk in range(4):
+            cols = slice(chunk * 256, chunk * 256 + 256)
+            sums = dot(pres_hl[:, near], diff_l[near, cols]) + dot(pres_hl[:, places], diff_l[places, cols])
+            grad_l[:, cols] = grad_l[:, cols] + halves(sums)
         receive_group(first, 1, pres_hl, C)
         places = group_places(1, C)
+        products = [dot(pres_hl[:, places], diff_l[places, chunk * 256:chunk * 256 + 256]) for chunk in range(4)]
+        moved = []
         for chunk in range(4):
             cols = slice(chunk * 256, chunk * 256 + 256)
-            gradient = grad_l[:, cols] + halves(dot(pres_hl[:, places], diff_l[places, cols]))
-            moved = vel_l[:, cols] - rows_l[6:7, cols] * gradient
-            vel_l[:, cols] = moved
-            put_pieces(second, chunk, moved)
-            send(second, (2 * chunk, 2 * chunk + 1))
+            gradient = grad_l[:, cols] + halves(products[chunk])
+            moved.append(vel_l[:, cols] - rows_l[6:7, cols] * gradient)
+        put_and_send(second, moved)
+        for chunk in range(4):
+            vel_l[:, chunk * 256:chunk * 256 + 256] = moved[chunk]
 
         for chunk in range(4):
             cols = slice(chunk * 256, chunk * 256 + 256)
@@ -382,15 +382,16 @@
         def _():
             v_out[...] = vel[:L, :E]
 
-        def divergence(places):
-            wide = dot(vel_hl[:, places], weight[places, :])
+        def divergence(*ranges):
+            wide = sum(dot(vel_hl[:, places], weight[places, :]) for places in ranges)
             return halves(wide[:, :C] + wide[:, C:])
 
         right[...] = pres[...] - divergence(slice(0, EP))
+        each(range(8), lambda turn: copy(first, turn).wait_send())
+        each(range(8), lambda turn: copy(second, turn).wait_send())
         receive(second, 3, 2, vel_hl, EP)
-        right[...] = right[...] - divergence(slice(EP + 3 * H, EP + 5 * H))
         receive_group(second, 0, vel_hl, EP)
-        right[...] = right[...] - divergence(group_places(0, EP))
+        right[...] = right[...] - divergence(slice(EP + 3 * H, EP + 5 * H), group_places(0, EP))
         receive_group(second, 1, vel_hl, EP)
         to_columns(right[...] - divergence(group_places(1, EP)), solve_in)
         solve()
@@ -404,8 +405,6 @@
 
     lax.fori_loop(0, NSUB, substep, 0)
     p_out[...] = pres[:L, :]
-    for exchange in range(2 * NSUB):
-        each(range(8), lambda turn: copy(exchange, turn).wait_send())
 
 
 def store(p, v, p_out, v_out, sem):

time: 51.7 us -> 51.8 us (level)
  no operation moved by 1% of the time
where the time goes in v4:
time: 51.8 us; the launch traced here: 51.7 us
  Pallas kernels  51 us (98%)
  between operations  0.64 us (1%)
    pallas_call x1, Pallas kernels, on_device(): pl.pallas_call(functools.partial(kernel, n_lat, n_lon), out_shape=(vmem((...  50.3 us

profile of v4, /device:TPU:6, one launch (start us, length us, event | category | flops | bytes accessed | tf_op | source)
XLA Modules:
  0.0 51.7 jit_solution(11221460573805752386)
XLA Ops:
  0.6 50.3 %shard_map.113 = (f32[30,640]{1,0:T(8,128)S(1)}, f32[30,960]{1,0:T(8,128)S(1)}) custom-call(f32[30,1,640]{2,1,0:T(1,128)} %bitcast.8, f32[30,1,960]{2,1,0:T(1,128)} %bitcast.7, s32[1,2,960]{2,1,0:T(2,128)} %ec_hbm.1, s32[3,1,640]{2,1,0:T(1,128)} %bitcast.10, s32[1,8,128]{2,1,0:T(8,128)} %sc_hbm.1, s32[1,8,128]{2,1,0:T(8,128)} %se_hbm.1, f32[1,960]{1,0:T(1,128)} %inv_hbm.1, ...), custom_call_target="tpu_custom_call" | custom-call | tf_op jit(solution)/shard_map/pallas_call | solution.py:431
  51.0 0.7 %shard_map.114 = (f32[30,1,640]{2,1,0:T(1,128)}, f32[30,1,960]{2,1,0:T(1,128)}) custom-call(f32[30,640]{1,0:T(8,128)S(1)} %get-tuple-element.6.p, f32[30,960]{1,0:T(8,128)S(1)} %get-tuple-element.7.v), custom_call_target="tpu_custom_call" | custom-call | tf_op jit(solution)/shard_map/pallas_call | solution.py:458

commit v5 on v4

--- a/solution.py
+++ b/solution.py
@@ -42,7 +42,7 @@
     pres, vel, pieces_out, pieces_in,
     pres_hl, vel_hl, pick_c, pick_e, diff, diff_l, weight,
     rows_l, grad_l, vel_l, right, solve_in, solve_mid, coef_a, coef_b, coef_r,
-    in_sem, send_sem, recv_sem,
+    send_sem, recv_sem,
 ):
     a, b = lax.axis_index("lat"), lax.axis_index("lon")
     not_first, not_last = a > 0, a < n_lat - 1
@@ -69,7 +69,8 @@
             view = source
         else:
             view = source.at[0] if source.shape[0] == 1 else source.at[:, 0, :]
-        loads.append(pltpu.make_async_copy(view, target, in_sem.at[i]))
+        semaphore = send_sem.at[0, i] if i < 2 else send_sem.at[1, i - 2]
+        loads.append(pltpu.make_async_copy(view, target, semaphore))
     loads[0].start()
     loads[1].start()
 
@@ -91,8 +92,8 @@
         return pltpu.make_async_remote_copy(
             src_ref=pieces_out.at[exchange, turn],
             dst_ref=pieces_in.at[exchange, 7 - member],
-            send_sem=send_sem.at[exchange, turn],
-            recv_sem=recv_sem.at[exchange, 7 - member],
+            send_sem=send_sem.at[exchange % 2, turn],
+            recv_sem=recv_sem.at[exchange % 2, 7 - member],
             device_id=device_at(p, q),
             device_id_type=MESH,
         )
@@ -113,8 +114,8 @@
             pltpu.make_async_remote_copy(
                 src_ref=pieces_out.at[exchange, i],
                 dst_ref=pieces_in.at[exchange, first + i],
-                send_sem=send_sem.at[exchange, i],
-                recv_sem=recv_sem.at[exchange, first + i],
+                send_sem=send_sem.at[exchange % 2, i],
+                recv_sem=recv_sem.at[exchange % 2, first + i],
                 device_id=device_at(0, 1),
                 device_id_type=MESH,
             ).wait_recv()
@@ -125,17 +126,21 @@
             target[LP:LP + L, cols] = low
 
     ahead_first = 1 - lax.min(lax.rem(a, 4), 1)
+    farther = 5 - 5 * ahead_first
+    farther_there = jnp.where(ahead_first == 1, not_first, not_last)
     groups = (
-        (5 * ahead_first, jnp.where(ahead_first == 1, not_last, not_first)),
-        (5 - 5 * ahead_first, jnp.where(ahead_first == 1, not_first, not_last)),
+        (5 * ahead_first, 3, jnp.where(ahead_first == 1, not_last, not_first)),
+        (farther + 1 - core, 2, farther_there),
+        (farther + 2 * core, 1, farther_there),
     )
 
     def receive_group(exchange, group, target, base):
-        first, there = groups[group]
-        pl.when(there)(lambda: receive(exchange, first, 3, target, base))
+        first, count, there = groups[group]
+        pl.when(there)(lambda: receive(exchange, first, count, target, base))
 
     def group_places(group, base):
-        return pl.ds(pl.multiple_of(base + groups[group][0] * H, H), 3 * H)
+        first, count, _ = groups[group]
+        return pl.ds(pl.multiple_of(base + first * H, H), count * H)
 
     def in_blocks(count, build):
         def step(block, carry):
@@ -281,15 +286,18 @@
             pres_hl[:LP, block * H:(block + 1) * H] = high
             pres_hl[LP:, block * H:(block + 1) * H] = low
 
-    def put_and_send(exchange, chunks):
+    def put(exchange, chunks, then=lambda chunk: None):
         for chunk, x in enumerate(chunks):
             for half in range(2):
                 pieces_out[exchange, 2 * chunk + half] = x[:L, half * H:(half + 1) * H]
-            send(exchange, (2 * chunk, 2 * chunk + 1))
-
-    def pressure_pieces(exchange):
+            then(chunk)
+
+    def put_and_send(exchange, chunks):
+        put(exchange, chunks, lambda chunk: send(exchange, (2 * chunk, 2 * chunk + 1)))
+
+    def pressure_products():
         products = [dot(pres_hl[:, :C], pick_c[:, chunk * 256:chunk * 256 + 256]) for chunk in range(4)]
-        put_and_send(exchange, [halves(x) for x in products])
+        return [halves(x) for x in products]
 
     def own_gradient():
         for chunk in range(4):
@@ -305,8 +313,9 @@
     pres_hl[:LP, :C] = high
     pres_hl[LP:, :C] = low
     pres_hl[:, C:] = jnp.zeros((2 * LP, N), BF16)
+    put(0, pressure_products())
     pl.semaphore_wait(barrier, 2 + 3 * lax.min(a, 1) + 3 * lax.min(n_lat - 1 - a, 1))
-    pressure_pieces(0)
+    send(0, range(8))
 
     loads[2].wait()
     build_pick(se_in, pick_e, EP)
@@ -354,6 +363,11 @@
             grad_l[:, cols] = grad_l[:, cols] + halves(sums)
         receive_group(first, 1, pres_hl, C)
         places = group_places(1, C)
+        for chunk in range(4):
+            cols = slice(chunk * 256, chunk * 256 + 256)
+            grad_l[:, cols] = grad_l[:, cols] + halves(dot(pres_hl[:, places], diff_l[places, cols]))
+        receive_group(first, 2, pres_hl, C)
+        places = group_places(2, C)
         products = [dot(pres_hl[:, places], diff_l[places, chunk * 256:chunk * 256 + 256]) for chunk in range(4)]
         moved = []
         for chunk in range(4):
@@ -393,12 +407,14 @@
         receive_group(second, 0, vel_hl, EP)
         right[...] = right[...] - divergence(slice(EP + 3 * H, EP + 5 * H), group_places(0, EP))
         receive_group(second, 1, vel_hl, EP)
-        to_columns(right[...] - divergence(group_places(1, EP)), solve_in)
+        right[...] = right[...] - divergence(group_places(1, EP))
+        receive_group(second, 2, vel_hl, EP)
+        to_columns(right[...] - divergence(group_places(2, EP)), solve_in)
         solve()
 
         @pl.when(s < NSUB - 1)
         def _():
-            pressure_pieces(second + 1)
+            put_and_send(second + 1, pressure_products())
             own_gradient()
 
         return carry
@@ -448,8 +464,7 @@
                 vmem((8, N), F32), vmem((LP, N), F32), vmem((LP, N), F32), vmem((LP, C), F32),
                 vmem((8 * LP, H), F32), vmem((8 * LP, H), F32),
                 vmem((8 * LP, H), F32), vmem((8 * LP, H), F32), vmem((8 * LP, H), F32),
-                pltpu.SemaphoreType.DMA((10,)),
-                pltpu.SemaphoreType.DMA((2 * NSUB, 8)), pltpu.SemaphoreType.DMA((2 * NSUB, 8)),
+                pltpu.SemaphoreType.DMA((2, 8)), pltpu.SemaphoreType.DMA((2, 8)),
             ],
             compiler_params=pltpu.CompilerParams(
                 collective_id=0, has_side_effects=True, vmem_limit_bytes=60 * 1024 * 1024

time: 51.8 us -> 50.3 us (0.971)
  Pallas kernels: 51 us -> 49.5 us
    pallas_call x1, Pallas kernels: 50.3 us -> 48.8 us  [on_device(): pl.pallas_call(functools.partial(kernel, n_lat, n_lon), out_shape=(vmem((...]
where the time goes in v5:
time: 50.3 us; the launch traced here: 50.1 us
  Pallas kernels  49.5 us (98%)
  between operations  0.64 us (1%)
    pallas_call x1, Pallas kernels, on_device(): pl.pallas_call(functools.partial(kernel, n_lat, n_lon), out_shape=(vmem((...  48.8 us

profile of v5, /device:TPU:6, one launch (start us, length us, event | category | flops | bytes accessed | tf_op | source)
XLA Modules:
  0.0 50.1 jit_solution(5840380138828637180)
XLA Ops:
  0.6 48.8 %shard_map.113 = (f32[30,640]{1,0:T(8,128)S(1)}, f32[30,960]{1,0:T(8,128)S(1)}) custom-call(f32[30,1,640]{2,1,0:T(1,128)} %bitcast.8, f32[30,1,960]{2,1,0:T(1,128)} %bitcast.7, s32[1,2,960]{2,1,0:T(2,128)} %ec_hbm.1, s32[3,1,640]{2,1,0:T(1,128)} %bitcast.10, s32[1,8,128]{2,1,0:T(8,128)} %sc_hbm.1, s32[1,8,128]{2,1,0:T(8,128)} %se_hbm.1, f32[1,960]{1,0:T(1,128)} %inv_hbm.1, ...), custom_call_target="tpu_custom_call" | custom-call | tf_op jit(solution)/shard_map/pallas_call | solution.py:447
  49.4 0.7 %shard_map.114 = (f32[30,1,640]{2,1,0:T(1,128)}, f32[30,1,960]{2,1,0:T(1,128)}) custom-call(f32[30,640]{1,0:T(8,128)S(1)} %get-tuple-element.6.p, f32[30,960]{1,0:T(8,128)S(1)} %get-tuple-element.7.v), custom_call_target="tpu_custom_call" | custom-call | tf_op jit(solution)/shard_map/pallas_call | solution.py:473

commit v6 on v5

--- a/solution.py
+++ b/solution.py
@@ -69,7 +69,7 @@
             view = source
         else:
             view = source.at[0] if source.shape[0] == 1 else source.at[:, 0, :]
-        semaphore = send_sem.at[0, i] if i < 2 else send_sem.at[1, i - 2]
+        semaphore = send_sem.at[i] if i < 2 else recv_sem.at[1, i - 2]
         loads.append(pltpu.make_async_copy(view, target, semaphore))
     loads[0].start()
     loads[1].start()
@@ -92,7 +92,7 @@
         return pltpu.make_async_remote_copy(
             src_ref=pieces_out.at[exchange, turn],
             dst_ref=pieces_in.at[exchange, 7 - member],
-            send_sem=send_sem.at[exchange % 2, turn],
+            send_sem=send_sem.at[exchange % 2],
             recv_sem=recv_sem.at[exchange % 2, 7 - member],
             device_id=device_at(p, q),
             device_id_type=MESH,
@@ -114,7 +114,7 @@
             pltpu.make_async_remote_copy(
                 src_ref=pieces_out.at[exchange, i],
                 dst_ref=pieces_in.at[exchange, first + i],
-                send_sem=send_sem.at[exchange % 2, i],
+                send_sem=send_sem.at[exchange % 2],
                 recv_sem=recv_sem.at[exchange % 2, first + i],
                 device_id=device_at(0, 1),
                 device_id_type=MESH,
@@ -141,6 +141,21 @@
     def group_places(group, base):
         first, count, _ = groups[group]
         return pl.ds(pl.multiple_of(base + first * H, H), count * H)
+
+    def wait_sent(exchange):
+        def wait_for(count):
+            pltpu.make_async_remote_copy(
+                src_ref=pieces_out.at[exchange, pl.ds(0, count)],
+                dst_ref=pieces_in.at[exchange, pl.ds(0, count)],
+                send_sem=send_sem.at[exchange % 2],
+                recv_sem=recv_sem.at[exchange % 2, 0],
+                device_id=device_at(0, 1),
+                device_id_type=MESH,
+            ).wait_send()
+
+        inside = not_first & not_last
+        pl.when(inside)(lambda: wait_for(8))
+        pl.when(jnp.logical_not(inside))(lambda: wait_for(5 if n_lat > 1 else 2))
 
     def in_blocks(count, build):
         def step(block, carry):
@@ -286,18 +301,20 @@
             pres_hl[:LP, block * H:(block + 1) * H] = high
             pres_hl[LP:, block * H:(block + 1) * H] = low
 
-    def put(exchange, chunks, then=lambda chunk: None):
-        for chunk, x in enumerate(chunks):
-            for half in range(2):
-                pieces_out[exchange, 2 * chunk + half] = x[:L, half * H:(half + 1) * H]
-            then(chunk)
-
-    def put_and_send(exchange, chunks):
-        put(exchange, chunks, lambda chunk: send(exchange, (2 * chunk, 2 * chunk + 1)))
-
-    def pressure_products():
-        products = [dot(pres_hl[:, :C], pick_c[:, chunk * 256:chunk * 256 + 256]) for chunk in range(4)]
-        return [halves(x) for x in products]
+    def put(exchange, chunk, x):
+        for half in range(2):
+            pieces_out[exchange, 2 * chunk + half] = x[:L, half * H:(half + 1) * H]
+
+    def pressure_product(chunk):
+        return dot(pres_hl[:, :C], pick_c[:, chunk * 256:chunk * 256 + 256])
+
+    def send_pressure(exchange):
+        ready = [pressure_product(0), pressure_product(1)]
+        for chunk in range(4):
+            put(exchange, chunk, halves(ready[chunk]))
+            send(exchange, (2 * chunk, 2 * chunk + 1))
+            if chunk == 0:
+                ready += [pressure_product(2), pressure_product(3)]
 
     def own_gradient():
         for chunk in range(4):
@@ -313,14 +330,14 @@
     pres_hl[:LP, :C] = high
     pres_hl[LP:, :C] = low
     pres_hl[:, C:] = jnp.zeros((2 * LP, N), BF16)
-    put(0, pressure_products())
+    for load in loads[2:]:
+        load.wait()
+    for chunk in range(4):
+        put(0, chunk, halves(pressure_product(chunk)))
     pl.semaphore_wait(barrier, 2 + 3 * lax.min(a, 1) + 3 * lax.min(n_lat - 1 - a, 1))
     send(0, range(8))
 
-    loads[2].wait()
     build_pick(se_in, pick_e, EP)
-    for i in range(3, 10):
-        loads[i].wait()
     vel[...] = jnp.zeros_like(vel)
     vel[:L, :E] = v_in[...]
     high, low = split(vel[...])
@@ -374,7 +391,9 @@
             cols = slice(chunk * 256, chunk * 256 + 256)
             gradient = grad_l[:, cols] + halves(products[chunk])
             moved.append(vel_l[:, cols] - rows_l[6:7, cols] * gradient)
-        put_and_send(second, moved)
+        for chunk in range(4):
+            put(second, chunk, moved[chunk])
+            send(second, (2 * chunk, 2 * chunk + 1))
         for chunk in range(4):
             vel_l[:, chunk * 256:chunk * 256 + 256] = moved[chunk]
 
@@ -401,8 +420,8 @@
             return halves(wide[:, :C] + wide[:, C:])
 
         right[...] = pres[...] - divergence(slice(0, EP))
-        each(range(8), lambda turn: copy(first, turn).wait_send())
-        each(range(8), lambda turn: copy(second, turn).wait_send())
+        wait_sent(first)
+        wait_sent(second)
         receive(second, 3, 2, vel_hl, EP)
         receive_group(second, 0, vel_hl, EP)
         right[...] = right[...] - divergence(slice(EP + 3 * H, EP + 5 * H), group_places(0, EP))
@@ -414,7 +433,7 @@
 
         @pl.when(s < NSUB - 1)
         def _():
-            put_and_send(second + 1, pressure_products())
+            send_pressure(second + 1)
             own_gradient()
 
         return carry
@@ -464,7 +483,7 @@
                 vmem((8, N), F32), vmem((LP, N), F32), vmem((LP, N), F32), vmem((LP, C), F32),
                 vmem((8 * LP, H), F32), vmem((8 * LP, H), F32),
                 vmem((8 * LP, H), F32), vmem((8 * LP, H), F32), vmem((8 * LP, H), F32),
-                pltpu.SemaphoreType.DMA((2, 8)), pltpu.SemaphoreType.DMA((2, 8)),
+                pltpu.SemaphoreType.DMA((2,)), pltpu.SemaphoreType.DMA((2, 8)),
             ],
             compiler_params=pltpu.CompilerParams(
                 collective_id=0, has_side_effects=True, vmem_limit_bytes=60 * 1024 * 1024

time: 50.3 us -> 50.1 us (level)
  no operation moved by 1% of the time
where the time goes in v6:
time: 50.1 us; the launch traced here: 50 us
  Pallas kernels  49.3 us (98%)
  between operations  0.64 us (1%)
    pallas_call x1, Pallas kernels, on_device(): pl.pallas_call(functools.partial(kernel, n_lat, n_lon), out_shape=(vmem((...  48.6 us

profile of v6, /device:TPU:6, one launch (start us, length us, event | category | flops | bytes accessed | tf_op | source)
XLA Modules:
  0.0 50.0 jit_solution(2594919528245552712)
XLA Ops:
  0.6 48.6 %shard_map.113 = (f32[30,640]{1,0:T(8,128)S(1)}, f32[30,960]{1,0:T(8,128)S(1)}) custom-call(f32[30,1,640]{2,1,0:T(1,128)} %bitcast.8, f32[30,1,960]{2,1,0:T(1,128)} %bitcast.7, s32[1,2,960]{2,1,0:T(2,128)} %ec_hbm.1, s32[3,1,640]{2,1,0:T(1,128)} %bitcast.10, s32[1,8,128]{2,1,0:T(8,128)} %sc_hbm.1, s32[1,8,128]{2,1,0:T(8,128)} %se_hbm.1, f32[1,960]{1,0:T(1,128)} %inv_hbm.1, ...), custom_call_target="tpu_custom_call" | custom-call | tf_op jit(solution)/shard_map/pallas_call | solution.py:466
  49.3 0.7 %shard_map.114 = (f32[30,1,640]{2,1,0:T(1,128)}, f32[30,1,960]{2,1,0:T(1,128)}) custom-call(f32[30,640]{1,0:T(8,128)S(1)} %get-tuple-element.6.p, f32[30,960]{1,0:T(8,128)S(1)} %get-tuple-element.7.v), custom_call_target="tpu_custom_call" | custom-call | tf_op jit(solution)/shard_map/pallas_call | solution.py:492
